TPU v7x, 512 devices: a whole 4x8x8 slice. The times are simulated.
512 devices in a mesh: pts: 32 (over y, x), cen: 16 (over z, core).
Axes of the slice: x: 4, y: 8, z: 8, core: 2. Of those that a mesh axis runs over, the one named last changes fastest.
Arguments:
- points: bfloat16 [131072, 1024], P('pts'), may hold values from -60 to 60
- fine_assign: int32 [2, 131072], P(None, 'pts'), may hold values from 0 to 2047
- fine_start: float32 [2048, 1024], P('cen'), may hold values from -3 to 3
- coarse_start: float32 [64, 1024], replicated, may hold values from -3 to 3
- coarse_assign: int32 [2048], P('cen'), may hold values from 0 to 63
Outputs:
- fine_centroids: float32 [2048, 1024], P('cen')
- coarse_centroids: float32 [64, 1024], replicated
- gaps: float32 [2, 131072], P(None, 'pts')
All inputs are finite; a program needn't handle non-finite values.
Results may differ from a plain program's by a relative error of at most 0.0028.
Values sent between devices are 32-bit elements; how exact they have to be, the bound alone decides.
A program may use at most 64 MiB of HBM per device.

v0:
```python
import math

import jax
import jax.numpy as jnp
from jax import lax
from jax.sharding import PartitionSpec as P

NC = 64
PASSES = 2


prior_weight = 4.0


def copy_for_each(x, axis):
    size = lax.axis_size(axis)
    return lax.all_to_all(jnp.broadcast_to(x[None], (size, *x.shape)), axis, 0, 0, tiled=True)


def over_copies(x, axis):
    everything = copy_for_each(x, axis)
    return jnp.sum(everything, axis=0)


def over_copies_2(x, axis):
    everything = copy_for_each(x, axis)
    return jnp.min(everything, axis=0)


def in_blocks(x, dim, size):
    before, after = (x.shape[:dim], x.shape[dim + 1 :])
    return jnp.moveaxis(x.reshape(*before, size, -1, *after), dim, 0)


def sum_at_owner(x, axis, dim):
    blocks = in_blocks(x, dim, lax.axis_size(axis))
    arrived = lax.all_to_all(blocks, axis, split_axis=0, concat_axis=0, tiled=True)
    return arrived.sum(axis=0)


def in_one(arrays, axis):
    ends = [0]
    for a in arrays:
        ends.append(ends[-1] + a.size)
    running = over_copies(jnp.concatenate([a.ravel() for a in arrays]), axis)
    return tuple((running[b:e].reshape(a.shape) for a, b, e in zip(arrays, ends, ends[1:])))


def rows_first(arrays, axis, dims):
    turned = [jnp.moveaxis(a, dim, 0) for a, dim in zip(arrays, dims)]
    widths = [t[0].size for t in turned]
    both = jnp.concatenate([t.reshape(-1, w) for t, w in zip(turned, widths)], axis=1)
    filled = lax.all_gather(both, axis, axis=0, tiled=True)
    blocks = jnp.split(filled, [sum(widths[:k]) for k in range(1, len(widths))], axis=1)
    return tuple(
        (
            jnp.moveaxis(b.reshape(-1, *t.shape[1:]), 0, dim)
            for b, t, dim in zip(blocks, turned, dims)
        )
    )


def refine(totals, counts, coarse_cols, coarse_table):
    lookup = jnp.dot(coarse_table, coarse_cols, precision=lax.Precision.HIGHEST)
    fine_next = (totals + prior_weight * lookup) / (counts + prior_weight)[:, None]
    coarse_part = lax.dot_general(
        coarse_table,
        counts[:, None] * fine_next,
        (((0,), (0,)), ((), ())),
        precision=lax.Precision.HIGHEST,
    )
    coarse_weight = jnp.sum(coarse_table * counts[:, None], axis=0)
    return (fine_next, coarse_part, coarse_weight)


def on_device(points, fine_assign, fine_start, coarse_start, coarse_assign):
    width = points.shape[1]
    local_count = fine_start.shape[0]
    offset = lax.axis_index("cen") * local_count
    columns = jnp.arange(local_count, dtype=jnp.int32)
    coarse_table = (coarse_assign[:, None] == jnp.arange(NC, dtype=jnp.int32)[None, :]).astype(
        jnp.float32
    )
    point_values = points.astype(jnp.float32)
    squares = jnp.sum(point_values * point_values, axis=1)
    fine_now = fine_start
    coarse_now = coarse_start
    gap_rows = []
    for pass_index in range(PASSES):
        member = (fine_assign[pass_index] - offset)[:, None] == columns[None, :]
        products = jnp.dot(
            points, fine_now.astype(jnp.bfloat16).T, preferred_element_type=jnp.float32
        )
        energy = jnp.sum(fine_now * fine_now, axis=1)[None, :] - 2.0 * products
        picked_local = jnp.sum(jnp.where(member, energy, 0.0), axis=1)
        nearest_local = jnp.min(energy, axis=1)
        picked = over_copies(picked_local, "cen")
        nearest = over_copies_2(nearest_local, "cen")
        gap_rows.append((picked - nearest) / math.sqrt(width))
        weights = 1.0 / (1.0 + (squares + picked) / width)
        scaled = (point_values * weights[:, None]).astype(jnp.bfloat16)
        partial_sums = lax.dot_general(
            member.astype(jnp.bfloat16),
            scaled,
            (((0,), (0,)), ((), ())),
            preferred_element_type=jnp.float32,
        )
        partial_weights = jnp.sum(jnp.where(member, weights[:, None], 0.0), axis=0)
        share_width = width // lax.axis_size("pts")
        start = lax.axis_index("pts") * share_width
        shares = sum_at_owner(partial_sums, "pts", 1)
        counts = over_copies(partial_weights, "pts")
        coarse_cols = lax.dynamic_slice_in_dim(coarse_now, start, share_width, 1)
        fine_share, coarse_part, coarse_weight = refine(shares, counts, coarse_cols, coarse_table)
        coarse_sum, coarse_count = in_one((coarse_part, coarse_weight), "cen")
        coarse_share = (coarse_sum + prior_weight * coarse_cols) / (coarse_count + prior_weight)[
            :, None
        ]
        fine_now, coarse_now = rows_first((fine_share, coarse_share), "pts", (1, 1))
    return (fine_now, coarse_now, jnp.stack(gap_rows))


def solution(mesh):
    placed = (P("pts", None), P(None, "pts"), P("cen", None), P(), P("cen"))
    return jax.shard_map(
        on_device,
        mesh=mesh,
        in_specs=placed,
        out_specs=(P("cen", None), P(), P(None, "pts")),
        check_vma=False,
    )
```

profile of v0, /device:TPU:2, one launch (start us, length us, event | category | flops | bytes accessed | tf_op | source)
XLA Modules:
  0.0 298.8 jit_solution(10869809501321211903)
XLA Ops:
  0.6 1.2 multiply_reduce_fusion.1
  2.7 6.5 %fusion.33 = (f32[4096]{0:T(1024)S(1)}, f32[4096]{0:T(1024)S(1)}) fusion(s32[4096]{0:T(1024)S(1)} %bitcast.44, bf16[4096,1024]{1,0:T(8,128)(2,1)} %param.5, f32[128,1024]{1,0:T(8,128)} %param.7, f32[128]{0:T(128)S(1)} %multiply_reduce_fusion.1), kind=kOutput, calls=%fused_computation.70 | convolution fusion | flops 1077010432 | bytes 8962560 | tf_op jit(solution)/shard_map/dot_general | solution.py:91
  9.4 21.4 %all_to_all.58 = f32[16,1,4096]{2,1,0:T(1,128)S(1)} all-to-all(f32[16,1,4096]{2,1,0:T(1,128)S(1)} %broadcast_in_dim.46), channel_id=1, replica_groups=mesh['pts'=32,'cen'=16] {'cen'}, dimensions={0} | all-to-all | bytes 524288 | tf_op jit(solution)/shard_map/all_to_all | solution.py:17
  31.7 3.5 %all-to-all-start = ((f32[16,1,4096]{2,1,0:T(1,128)}), f32[16,1,4096]{2,1,0:T(1,128)S(1)}, u32[]{:S(2)}, u32[]{:S(2)}) async-start(f32[16,1,4096]{2,1,0:T(1,128)} %broadcast_in_dim.38), calls=%async_computation | async-start | bytes 524288 | tf_op jit(solution)/shard_map/all_to_all | solution.py:17
  35.2 5.1 %fusion = f32[4096]{0:T(1024)S(1)} fusion(bf16[4096,1024]{1,0:T(8,128)(2,1)} %param.5), kind=kLoop, calls=%fused_computation.3 | loop fusion | flops 12578816 | bytes 8404992 | tf_op jit(solution)/shard_map/reduce_sum | solution.py:85
  40.5 6.0 %all-to-all-done = f32[16,1,4096]{2,1,0:T(1,128)S(1)} async-done(((f32[16,1,4096]{2,1,0:T(1,128)}), f32[16,1,4096]{2,1,0:T(1,128)S(1)}, u32[]{:S(2)}, u32[]{:S(2)}) %all-to-all-start) | async-done | bytes 262176 | tf_op jit(solution)/shard_map/all_to_all | solution.py:17
  47.7 10.2 %all-to-all-start.2 = ((f32[32,1,128]{2,1,0:T(1,128)}), f32[32,1,128]{2,1,0:T(1,128)S(1)}, u32[]{:S(2)}, u32[]{:S(2)}) async-start(f32[32,1,128]{2,1,0:T(1,128)} %broadcast_in_dim.40), calls=%async_computation.2 | async-start | bytes 32768 | tf_op jit(solution)/shard_map/all_to_all | solution.py:17
  58.0 8.1 %fusion.5 = f32[128,1024]{0,1:T(8,128)} fusion(bf16[4096,1024]{1,0:T(8,128)(2,1)} %param.5, f32[4096]{0:T(1024)S(1)} %get-tuple-element.20, s32[4096]{0:T(1024)S(1)} %bitcast.46), kind=kOutput, calls=%fused_computation.7 | convolution fusion | flops 1086849024 | bytes 8945664 | tf_op jit(solution)/shard_map/dot_general | solution.py:102
  66.5 9.4 %all-to-all-start.1 = ((f32[32,128,32]{1,2,0:T(8,128)}), f32[32,128,32]{1,2,0:T(8,128)S(1)}, u32[]{:S(2)}, u32[]{:S(2)}) async-start(f32[32,128,32]{1,2,0:T(8,128)} %bitcast.3), calls=%async_computation.1 | async-start | bytes 1048576 | tf_op jit(solution)/shard_map/all_to_all | solution.py:37
  76.1 16.8 %all-to-all-done.1 = f32[32,128,32]{1,2,0:T(8,128)S(1)} async-done(((f32[32,128,32]{1,2,0:T(8,128)}), f32[32,128,32]{1,2,0:T(8,128)S(1)}, u32[]{:S(2)}, u32[]{:S(2)}) %all-to-all-start.1) | async-done | bytes 524320 | tf_op jit(solution)/shard_map/all_to_all | solution.py:37
  94.1 3.5 %all-to-all-start.3 = ((f32[16,1,2112]{2,1,0:T(1,128)}), f32[16,1,2112]{2,1,0:T(1,128)S(1)}, u32[]{:S(2)}, u32[]{:S(2)}) async-start(f32[16,1,2112]{2,1,0:T(1,128)} %broadcast_in_dim.41), calls=%async_computation.3 | async-start | bytes 278528 | tf_op jit(solution)/shard_map/all_to_all | solution.py:17
  97.7 8.7 %all-to-all-done.3 = f32[16,1,2112]{2,1,0:T(1,128)S(1)} async-done(((f32[16,1,2112]{2,1,0:T(1,128)}), f32[16,1,2112]{2,1,0:T(1,128)S(1)}, u32[]{:S(2)}, u32[]{:S(2)}) %all-to-all-start.3) | async-done | bytes 135200 | tf_op jit(solution)/shard_map/all_to_all | solution.py:17
  106.7 48.5 %all_gather.6 = f32[1024,192]{1,0:T(8,128)S(1)} all-gather(f32[32,192]{1,0:T(8,128)S(1)} %pad_maximum_fusion), channel_id=1, replica_groups=mesh['pts'=32,'cen'=16] {'pts'}, dimensions={0}, use_global_device_ids=true | all-gather | bytes 811008 | tf_op jit(solution)/shard_map/all_gather | solution.py:53
  155.4 6.5 %fusion.11 = (f32[4096]{0:T(1024)S(1)}, f32[128,4096]{1,0:T(8,128)S(1)}) fusion(s32[4096]{0:T(1024)S(1)} %bitcast.35, bf16[4096,1024]{1,0:T(8,128)(2,1)} %param.5, f32[1024,192]{1,0:T(8,128)S(1)} %all_gather.6, f32[128]{0:T(128)S(1)} %multiply_reduce_fusion), kind=kOutput, calls=%fused_computation.15 | convolution fusion | flops 1076359168 | bytes 10781184 | tf_op jit(solution)/shard_map/dot_general | solution.py:91
  162.2 14.1 %all_to_all.59 = f32[16,1,4096]{2,1,0:T(1,128)S(1)} all-to-all(f32[16,1,4096]{2,1,0:T(1,128)S(1)} %broadcast_in_dim.47), channel_id=1, replica_groups=mesh['pts'=32,'cen'=16] {'cen'}, dimensions={0} | all-to-all | bytes 524288 | tf_op jit(solution)/shard_map/all_to_all | solution.py:17
  177.2 3.5 %all-to-all-start.4 = ((f32[16,1,4096]{2,1,0:T(1,128)}), f32[16,1,4096]{2,1,0:T(1,128)S(1)}, u32[]{:S(2)}, u32[]{:S(2)}) async-start(f32[16,1,4096]{2,1,0:T(1,128)} %broadcast_in_dim.42), calls=%async_computation.4 | async-start | bytes 524288 | tf_op jit(solution)/shard_map/all_to_all | solution.py:17
  180.9 11.1 %all-to-all-done.4 = f32[16,1,4096]{2,1,0:T(1,128)S(1)} async-done(((f32[16,1,4096]{2,1,0:T(1,128)}), f32[16,1,4096]{2,1,0:T(1,128)S(1)}, u32[]{:S(2)}, u32[]{:S(2)}) %all-to-all-start.4) | async-done | bytes 262176 | tf_op jit(solution)/shard_map/all_to_all | solution.py:17
  193.2 6.6 %all-to-all-start.6 = ((f32[32,1,128]{2,1,0:T(1,128)}), f32[32,1,128]{2,1,0:T(1,128)S(1)}, u32[]{:S(2)}, u32[]{:S(2)}) async-start(f32[32,1,128]{2,1,0:T(1,128)} %broadcast_in_dim.44), calls=%async_computation.6 | async-start | bytes 32768 | tf_op jit(solution)/shard_map/all_to_all | solution.py:17
  199.9 8.1 %fusion.3 = f32[128,1024]{0,1:T(8,128)} fusion(bf16[4096,1024]{1,0:T(8,128)(2,1)} %param.5, f32[4096]{0:T(1024)S(1)} %get-tuple-element.22, s32[4096]{0:T(1024)S(1)} %bitcast.37), kind=kOutput, calls=%fused_computation.6 | convolution fusion | flops 1086849024 | bytes 8945664 | tf_op jit(solution)/shard_map/dot_general | solution.py:102
  208.3 9.4 %all-to-all-start.5 = ((f32[32,128,32]{1,2,0:T(8,128)}), f32[32,128,32]{1,2,0:T(8,128)S(1)}, u32[]{:S(2)}, u32[]{:S(2)}) async-start(f32[32,128,32]{1,2,0:T(8,128)} %bitcast.9), calls=%async_computation.5 | async-start | bytes 1048576 | tf_op jit(solution)/shard_map/all_to_all | solution.py:37
  217.9 16.8 %all-to-all-done.5 = f32[32,128,32]{1,2,0:T(8,128)S(1)} async-done(((f32[32,128,32]{1,2,0:T(8,128)}), f32[32,128,32]{1,2,0:T(8,128)S(1)}, u32[]{:S(2)}, u32[]{:S(2)}) %all-to-all-start.5) | async-done | bytes 524320 | tf_op jit(solution)/shard_map/all_to_all | solution.py:37
  235.9 3.5 %all-to-all-start.7 = ((f32[16,1,2112]{2,1,0:T(1,128)}), f32[16,1,2112]{2,1,0:T(1,128)S(1)}, u32[]{:S(2)}, u32[]{:S(2)}) async-start(f32[16,1,2112]{2,1,0:T(1,128)} %broadcast_in_dim.45), calls=%async_computation.7 | async-start | bytes 278528 | tf_op jit(solution)/shard_map/all_to_all | solution.py:17
  240.1 8.1 %all-to-all-done.7 = f32[16,1,2112]{2,1,0:T(1,128)S(1)} async-done(((f32[16,1,2112]{2,1,0:T(1,128)}), f32[16,1,2112]{2,1,0:T(1,128)S(1)}, u32[]{:S(2)}, u32[]{:S(2)}) %all-to-all-start.7) | async-done | bytes 135200 | tf_op jit(solution)/shard_map/all_to_all | solution.py:17
  248.5 48.3 %all_gather.7 = f32[1024,192]{1,0:T(8,128)S(1)} all-gather(f32[32,192]{1,0:T(8,128)S(1)} %pad_maximum_fusion.1), channel_id=1, replica_groups=mesh['pts'=32,'cen'=16] {'pts'}, dimensions={0}, use_global_device_ids=true | all-gather | bytes 811008 | tf_op jit(solution)/shard_map/all_gather | solution.py:53
  (63 shorter events, 12.7 us)
Async XLA Ops:
  0.6 75.3 %copy-start = (f32[64,1024]{1,0:T(8,128)S(1)}, f32[64,1024]{1,0:T(8,128)}, u32[]{:S(2)}) copy-start(f32[64,1024]{1,0:T(8,128)} %param.8) | copy-start | bytes 786436
  31.7 14.9 %all-to-all-start = ((f32[16,1,4096]{2,1,0:T(1,128)}), f32[16,1,4096]{2,1,0:T(1,128)S(1)}, u32[]{:S(2)}, u32[]{:S(2)}) async-start(f32[16,1,4096]{2,1,0:T(1,128)} %broadcast_in_dim.38), calls=%async_computation | async-start | bytes 524288 | tf_op jit(solution)/shard_map/all_to_all | solution.py:17
  47.7 18.7 %all-to-all-start.2 = ((f32[32,1,128]{2,1,0:T(1,128)}), f32[32,1,128]{2,1,0:T(1,128)S(1)}, u32[]{:S(2)}, u32[]{:S(2)}) async-start(f32[32,1,128]{2,1,0:T(1,128)} %broadcast_in_dim.40), calls=%async_computation.2 | async-start | bytes 32768 | tf_op jit(solution)/shard_map/all_to_all | solution.py:17
  58.0 18.0 %copy-start.1 = (s32[128]{0:T(128)S(1)}, s32[128]{0:T(128)}, u32[]{:S(2)}) copy-start(s32[128]{0:T(128)} %param.9) | copy-start | bytes 1540
  66.5 26.4 %all-to-all-start.1 = ((f32[32,128,32]{1,2,0:T(8,128)}), f32[32,128,32]{1,2,0:T(8,128)S(1)}, u32[]{:S(2)}, u32[]{:S(2)}) async-start(f32[32,128,32]{1,2,0:T(8,128)} %bitcast.3), calls=%async_computation.1 | async-start | bytes 1048576 | tf_op jit(solution)/shard_map/all_to_all | solution.py:37
  94.1 12.3 %all-to-all-start.3 = ((f32[16,1,2112]{2,1,0:T(1,128)}), f32[16,1,2112]{2,1,0:T(1,128)S(1)}, u32[]{:S(2)}, u32[]{:S(2)}) async-start(f32[16,1,2112]{2,1,0:T(1,128)} %broadcast_in_dim.41), calls=%async_computation.3 | async-start | bytes 278528 | tf_op jit(solution)/shard_map/all_to_all | solution.py:17
  177.2 14.9 %all-to-all-start.4 = ((f32[16,1,4096]{2,1,0:T(1,128)}), f32[16,1,4096]{2,1,0:T(1,128)S(1)}, u32[]{:S(2)}, u32[]{:S(2)}) async-start(f32[16,1,4096]{2,1,0:T(1,128)} %broadcast_in_dim.42), calls=%async_computation.4 | async-start | bytes 524288 | tf_op jit(solution)/shard_map/all_to_all | solution.py:17
  193.2 15.1 %all-to-all-start.6 = ((f32[32,1,128]{2,1,0:T(1,128)}), f32[32,1,128]{2,1,0:T(1,128)S(1)}, u32[]{:S(2)}, u32[]{:S(2)}) async-start(f32[32,1,128]{2,1,0:T(1,128)} %broadcast_in_dim.44), calls=%async_computation.6 | async-start | bytes 32768 | tf_op jit(solution)/shard_map/all_to_all | solution.py:17
  208.3 26.4 %all-to-all-start.5 = ((f32[32,128,32]{1,2,0:T(8,128)}), f32[32,128,32]{1,2,0:T(8,128)S(1)}, u32[]{:S(2)}, u32[]{:S(2)}) async-start(f32[32,128,32]{1,2,0:T(8,128)} %bitcast.9), calls=%async_computation.5 | async-start | bytes 1048576 | tf_op jit(solution)/shard_map/all_to_all | solution.py:37
  235.9 12.3 %all-to-all-start.7 = ((f32[16,1,2112]{2,1,0:T(1,128)}), f32[16,1,2112]{2,1,0:T(1,128)S(1)}, u32[]{:S(2)}, u32[]{:S(2)}) async-start(f32[16,1,2112]{2,1,0:T(1,128)} %broadcast_in_dim.45), calls=%async_computation.7 | async-start | bytes 278528 | tf_op jit(solution)/shard_map/all_to_all | solution.py:17
where the time goes:
time: 300 us; the launch traced here: 299 us
  blocking collectives  132 us (44%)
  waiting for transfers between devices  68.4 us (23%)
  starting transfers between devices  49.8 us (17%)
  matrix products  29.8 us (10%)
  other arithmetic  10.1 us (3%)
  local copies, waits for them, and re-layouts  7.5 us (2%)
    all_gather x2, blocking collectives, rows_first(): filled = lax.all_gather(both, axis, axis=0, tiled=True)  96.8 us
    all_to_all x2, blocking collectives, copy_for_each(): lax.all_to_all(jnp.broadcast_to(x[None], (size, *x.shape)), axis, 0, 0, t...  35.5 us
    all_to_all x6, waiting for transfers between devices, copy_for_each(): lax.all_to_all(jnp.broadcast_to(x[None], (size, *x.shape)), axis, 0, 0, t...  34.8 us
    all_to_all x2, waiting for transfers between devices, sum_at_owner(): lax.all_to_all(blocks, axis, split_axis=0, concat_axis=0, tiled=True)  33.6 us
    all_to_all x6, starting transfers between devices, copy_for_each(): lax.all_to_all(jnp.broadcast_to(x[None], (size, *x.shape)), axis, 0, 0, t...  31 us
    all_to_all x2, starting transfers between devices, sum_at_owner(): lax.all_to_all(blocks, axis, split_axis=0, concat_axis=0, tiled=True)  18.8 us
    dot_general x2, matrix products, on_device(): lax.dot_general(member.astype(jnp.bfloat16), scaled, (((0,), (0,)), ((),...  16.2 us
    dot_general x2, matrix products, on_device(): jnp.dot(points, fine_now.astype(jnp.bfloat16).T, preferred_element_type=j...  13 us
  transfers between devices with their start and end apart: 8, of which 8 were waited for; matrix products, arithmetic and copies ran while one was open for 8% of the time, Pallas kernels for 0%

commit v1 on v0

v1 whole, which is shorter than its diff:
```python
import jax
import jax.numpy as jnp
from jax import lax
from jax.experimental import pallas as pl
from jax.experimental.pallas import tpu as pltpu
from jax.sharding import PartitionSpec as P

NC = 64
PASSES = 2
PRIOR = 4.0
D = 1024
NP = 4096
NK = 128
NX, NY, NCEN = 4, 8, 16
CH = 512
STEPS = NP // CH
GP = NP // NCEN
F32 = jnp.float32
BF16 = jnp.bfloat16
MESH = pl.DeviceIdType.MESH
HIGH = lax.Precision.HIGHEST

FIRST = 8 + 128
ROWS = FIRST + 128


def dot_nt(a, b):
    return lax.dot_general(a, b, (((1,), (1,)), ((), ())), precision=HIGH, preferred_element_type=F32)


def kernel(
    points, assign, fine_start, coarse_start, coarse_assign,
    fine_out, coarse_out, gaps_out,
    xv, av, fv, cv, kv, in_sem,
    low, norm, squares, wv, cacc,
    ahead, hop_r, hop_l, blk_r, blk_l, got_l, got_r, ysend, yrecv,
    fine_g, cpack, crecv, coarse_g,
    pn, pn_recv, gap_g,
    rs_s, rs_r, ys_s, ys_r, gy_s, gy_r, gx_s, gx_r, cs_s, cs_r, cy_s, cy_r, cx_s, cx_r, p_s, p_r, g_s, g_r,
):
    pts = lax.axis_index("pts")
    cen = lax.axis_index("cen")
    y = pts // NX
    x = pts % NX
    x_right, x_left, x_far = (x + 1) % NX, (x + 3) % NX, (x + 2) % NX
    right = {"pts": y * NX + x_right}
    left = {"pts": y * NX + x_left}

    def y_peer(d):
        return {"pts": ((y + d) % NY) * NX + x}

    def c_peer(d):
        return {"cen": (cen + d) % NCEN}

    sends = []

    def remote(src, dst, s, r, where):
        copy = pltpu.make_async_remote_copy(
            src_ref=src, dst_ref=dst, send_sem=s, recv_sem=r, device_id=where, device_id_type=MESH
        )
        copy.start()
        sends.append(copy)
        return copy

    fine_in = pltpu.make_async_copy(fine_start, fv, in_sem.at[STEPS])
    fine_in.start()

    def x_copy(i):
        rows = pl.ds(pl.multiple_of(i * CH, CH), CH)
        return pltpu.make_async_copy(points.at[rows], xv.at[rows], in_sem.at[i])

    for i in range(STEPS):
        x_copy(i).start()
    a_in = pltpu.make_async_copy(assign, av, in_sem.at[STEPS + 1])
    k_in = pltpu.make_async_copy(coarse_assign, kv, in_sem.at[STEPS + 2])
    c_in = pltpu.make_async_copy(coarse_start, cv, in_sem.at[STEPS + 3])
    a_in.start()
    k_in.start()
    c_in.start()

    barrier = pltpu.get_barrier_semaphore()
    for where in [right, left] + [y_peer(d) for d in range(1, NY)] + [c_peer(d) for d in range(1, NCEN)]:
        pl.semaphore_signal(barrier, inc=1, device_id=where, device_id_type=MESH)

    fine_in.wait()
    total = jnp.zeros((1, NK), F32)
    for b in range(D // 128):
        t = fv[:, b * 128 : (b + 1) * 128].T
        low[b * 128 : (b + 1) * 128, :] = t.astype(BF16)
        total = total + jnp.sum(t * t, axis=0, keepdims=True)
    norm[...] = total
    a_in.wait()
    k_in.wait()
    c_in.wait()

    own = lax.broadcasted_iota(jnp.int32, (NK, CH), 0) + cen * NK

    def energies(p):
        cacc[...] = jnp.zeros_like(cacc)

        def body(i, carry):
            if p == 0:
                x_copy(i).wait()
            rows = pl.ds(pl.multiple_of(i * CH, CH), CH)
            xs = xv[rows, :]
            products = jnp.dot(xs, low[...], preferred_element_type=F32)
            energy = (norm[...] - 2.0 * products).T
            if p == 0:
                part = jnp.zeros((CH, 128), F32)
                for g in range(D // 128):
                    xf = xs[:, g * 128 : (g + 1) * 128].astype(F32)
                    part = part + xf * xf
                sq = jnp.sum(part.T, axis=0, keepdims=True)
                squares[i] = sq
            else:
                sq = squares[i]
            member = av[p : p + 1, rows] == own
            picked = jnp.sum(jnp.where(member, energy, 0.0), axis=0, keepdims=True)
            nearest = jnp.min(energy, axis=0, keepdims=True)
            weights = 1.0 / (1.0 + (sq + picked) / D)
            wm = jnp.where(member, weights, 0.0)
            high = wm.astype(BF16)
            wv[0:NK, rows] = high
            wv[NK : 2 * NK, rows] = (wm - high.astype(F32)).astype(BF16)
            for g in range(CH // 128):
                cacc[...] += wm[:, g * 128 : (g + 1) * 128]
            for g in range(CH // GP):
                pn[i * (CH // GP) + g, 2 * p : 2 * p + 1, :] = picked[:, g * GP : (g + 1) * GP]
                pn[i * (CH // GP) + g, 2 * p + 1 : 2 * p + 2, :] = nearest[:, g * GP : (g + 1) * GP]
            return carry

        lax.fori_loop(0, STEPS, body, 0)

    def block(b):
        cols = pl.multiple_of(b * 128, 128)
        rhs = jnp.concatenate([xv[:, pl.ds(cols, 128)], xv[:, pl.ds(512 + cols, 128)]], axis=1)
        both = jnp.dot(wv[...], rhs, preferred_element_type=F32)
        return (both[:NK] + both[NK:]).T

    share = x * NY + y
    turned = jnp.concatenate([cv[:, 0:512], cv[:, 512:1024]], axis=0).T
    cpack[...] = turned
    of = lax.broadcasted_iota(jnp.int32, (128, NK), 0)
    pick_a = (of == kv[...]).astype(F32)
    pick_b = (of == kv[...] + NC).astype(F32)
    coarse = cpack[pl.ds(pl.multiple_of(share * 16, 16), 16), :]

    pl.semaphore_wait(barrier, 2 + (NY - 1) + (NCEN - 1))

    for p in range(PASSES):
        last = p == PASSES - 1
        energies(p)
        if last:
            pn_copies = [
                remote(pn.at[(cen + d) % NCEN], pn_recv.at[d], p_s.at[d], p_r.at[d], c_peer(d))
                for d in range(1, NCEN)
            ]
        counts8 = jnp.sum(cacc[...].T.reshape(16, 8, NK), axis=0)

        t = block(x_far)
        ahead[p, 0:8, :] = counts8
        ahead[p, 8:ROWS, :] = t
        h1 = remote(ahead.at[p, 0:FIRST], hop_r.at[p], rs_s.at[p, 0], rs_r.at[p, 0], right)
        h2 = remote(ahead.at[p, FIRST:ROWS], hop_l.at[p], rs_s.at[p, 1], rs_r.at[p, 1], left)
        t = block(x_right)
        blk_r[p, FIRST:ROWS, :] = t[128:]
        r2 = remote(
            blk_r.at[p, FIRST:ROWS], got_l.at[p, FIRST:ROWS], rs_s.at[p, 2], rs_r.at[p, 2], right
        )
        blk_r[p, 0:8, :] = counts8
        blk_r[p, 8:FIRST, :] = t[:128]
        t = block(x_left)
        blk_l[p, 0:8, :] = counts8
        blk_l[p, 8:FIRST, :] = t[:128]
        l1 = remote(blk_l.at[p, 0:FIRST], got_r.at[p, 0:FIRST], rs_s.at[p, 3], rs_r.at[p, 3], left)
        h1.wait_recv()
        blk_r[p, 0:FIRST, :] += hop_r[p]
        r1 = remote(blk_r.at[p, 0:FIRST], got_l.at[p, 0:FIRST], rs_s.at[p, 4], rs_r.at[p, 4], right)
        h2.wait_recv()
        blk_l[p, FIRST:ROWS, :] = t[128:] + hop_l[p]
        l2 = remote(
            blk_l.at[p, FIRST:ROWS], got_r.at[p, FIRST:ROWS], rs_s.at[p, 5], rs_r.at[p, 5], left
        )
        t = block(x)
        for copy in (r2, l1, r1, l2):
            copy.wait_recv()
        counts8 = counts8 + got_l[p, 0:8, :] + got_r[p, 0:8, :]
        t = t + got_l[p, 8:ROWS, :] + got_r[p, 8:ROWS, :]
        for k in range(NY):
            ysend[p, k, 0:16, :] = t[k * 16 : (k + 1) * 16]
            ysend[p, k, 16:32, :] = t[128 + k * 16 : 128 + (k + 1) * 16]
            ysend[p, k, 32:40, :] = counts8
        ycopies = [
            remote(ysend.at[p, (y + d) % NY], yrecv.at[p, d], ys_s.at[p, d], ys_r.at[p, d], y_peer(d))
            for d in range(1, NY)
        ]
        if p > 0:
            coarse = coarse_update(ccopies, crecv, p - 1, coarse)
        lookup = jnp.concatenate(
            [
                jnp.dot(coarse, pick_a, precision=HIGH, preferred_element_type=F32),
                jnp.dot(coarse, pick_b, precision=HIGH, preferred_element_type=F32),
            ],
            axis=0,
        )
        if last:
            finish = pn[cen]
            picked0, near0, picked1, near1 = (finish[k : k + 1] for k in range(4))
            for d in range(1, NCEN):
                pn_copies[d - 1].wait_recv()
                picked0 = picked0 + pn_recv[d, 0:1, :]
                near0 = jnp.minimum(near0, pn_recv[d, 1:2, :])
                picked1 = picked1 + pn_recv[d, 2:3, :]
                near1 = jnp.minimum(near1, pn_recv[d, 3:4, :])
            gap_g[cen, 0:1, :] = (picked0 - near0) / 32.0
            gap_g[cen, 1:2, :] = (picked1 - near1) / 32.0
            gap_copies = [
                remote(gap_g.at[cen], gap_g.at[cen], g_s.at[d], g_r.at[d], c_peer(d)) for d in range(1, NCEN)
            ]
        all_sum = ysend[p, y]
        for d in range(1, NY):
            ycopies[d - 1].wait_recv()
            all_sum = all_sum + yrecv[p, d]
        counts = jnp.sum(all_sum[32:40], axis=0, keepdims=True)
        fine = (all_sum[0:32] + PRIOR * lookup) / (counts + PRIOR)
        fine_g[p, x, y] = fine
        gy = [
            remote(fine_g.at[p, x, y], fine_g.at[p, x, y], gy_s.at[p, d], gy_r.at[p, d], y_peer(d))
            for d in range(1, NY)
        ]
        weighted = counts * fine
        crecv[p, cen, 0:16, :] = dot_nt(weighted[0:16], pick_a) + dot_nt(weighted[16:32], pick_b)
        crecv[p, cen, 16:24, :] = dot_nt(jnp.broadcast_to(counts, (8, NK)), pick_a + pick_b)
        ccopies = [
            remote(crecv.at[p, cen], crecv.at[p, cen], cs_s.at[p, d], cs_r.at[p, d], c_peer(d))
            for d in range(1, NCEN)
        ]
        for copy in gy:
            copy.wait_recv()
        lo, hi = pl.ds(0, NY // 2), pl.ds(NY // 2, NY // 2)

        def to(where, half, sem):
            ref = fine_g.at[p, x, half]
            return remote(ref, ref, gx_s.at[p, sem], gx_r.at[p, sem], where)

        r_lo = to(right, lo, 0)
        l_hi = to(left, hi, 1)
        r_hi = to(right, hi, 2)
        l_lo = to(left, lo, 3)
        if last:
            coarse = coarse_update(ccopies, crecv, p, coarse)
            coarse_g[x, y] = coarse
            cy = [
                remote(coarse_g.at[x, y], coarse_g.at[x, y], cy_s.at[d], cy_r.at[d], y_peer(d))
                for d in range(1, NY)
            ]
        r_lo.wait_recv()
        ref = fine_g.at[p, x_left, lo]
        f_r = remote(ref, ref, gx_s.at[p, 4], gx_r.at[p, 4], right)
        l_hi.wait_recv()
        ref = fine_g.at[p, x_right, hi]
        f_l = remote(ref, ref, gx_s.at[p, 5], gx_r.at[p, 5], left)
        if last:
            for copy in cy:
                copy.wait_recv()

            def coarse_to(where, half, sem):
                ref = coarse_g.at[x, half]
                return remote(ref, ref, cx_s.at[sem], cx_r.at[sem], where)

            cr_lo = coarse_to(right, lo, 0)
            cl_hi = coarse_to(left, hi, 1)
            cr_hi = coarse_to(right, hi, 2)
            cl_lo = coarse_to(left, lo, 3)
            for d in range(1, NCEN):
                gap_copies[d - 1].wait_recv()
            for c in range(NCEN):
                gaps_out[:, c * GP : (c + 1) * GP] = gap_g[c]
        for copy in (r_hi, l_lo, f_r, f_l):
            copy.wait_recv()
        if last:
            cr_lo.wait_recv()
            ref = coarse_g.at[x_left, lo]
            cf_r = remote(ref, ref, cx_s.at[4], cx_r.at[4], right)
            cl_hi.wait_recv()
            ref = coarse_g.at[x_right, hi]
            cf_l = remote(ref, ref, cx_s.at[5], cx_r.at[5], left)
        total = jnp.zeros((1, NK), F32)
        for b in range(D // 128):
            h, bx = divmod(b, NX)
            t = fine_g[p, bx, :, h * 16 : (h + 1) * 16, :].reshape(128, NK)
            if last:
                fine_out[:, b * 128 : (b + 1) * 128] = t.T
            else:
                low[b * 128 : (b + 1) * 128, :] = t.astype(BF16)
                total = total + jnp.sum(t * t, axis=0, keepdims=True)
        if not last:
            norm[...] = total

    for copy in (cr_hi, cl_lo, cf_r, cf_l):
        copy.wait_recv()
    t = coarse_g[...].reshape(512, 128).T
    coarse_out[:, 0:512] = t[0:NC]
    coarse_out[:, 512:1024] = t[NC : 2 * NC]
    for copy in sends:
        copy.wait_send()


def coarse_update(copies, crecv, p, coarse):
    for copy in copies:
        copy.wait_recv()
    total = crecv[p, 0]
    for c in range(1, NCEN):
        total = total + crecv[p, c]
    return (total[0:16] + PRIOR * coarse) / (total[16:17] + PRIOR)


def on_device(points, fine_assign, fine_start, coarse_start, coarse_assign):
    dma = pltpu.SemaphoreType.DMA
    vmem = pltpu.VMEM
    n = PASSES
    scratch = [
        vmem((NP, D), BF16), vmem((PASSES, NP), jnp.int32), vmem((NK, D), F32), vmem((NC, D), F32),
        vmem((1, NK), jnp.int32), dma((STEPS + 4,)),
        vmem((D, NK), BF16), vmem((1, NK), F32), vmem((STEPS, 1, CH), F32), vmem((2 * NK, NP), BF16),
        vmem((NK, 128), F32),
        vmem((n, ROWS, 128), F32), vmem((n, FIRST, 128), F32), vmem((n, 128, 128), F32),
        vmem((n, ROWS, 128), F32), vmem((n, ROWS, 128), F32), vmem((n, ROWS, 128), F32), vmem((n, ROWS, 128), F32),
        vmem((n, NY, 40, 128), F32), vmem((n, NY, 40, 128), F32),
        vmem((n, NX, NY, 32, 128), F32), vmem((512, 128), F32), vmem((n, NCEN, 24, 128), F32),
        vmem((NX, NY, 16, 128), F32),
        vmem((NCEN, 4, GP), F32), vmem((NCEN, 4, GP), F32), vmem((NCEN, 2, GP), F32),
        dma((n, 6)), dma((n, 6)), dma((n, NY)), dma((n, NY)), dma((n, NY)), dma((n, NY)),
        dma((n, 6)), dma((n, 6)), dma((n, NCEN)), dma((n, NCEN)), dma((NY,)), dma((NY,)),
        dma((6,)), dma((6,)), dma((NCEN,)), dma((NCEN,)), dma((NCEN,)), dma((NCEN,)),
    ]
    return tuple(pl.pallas_call(
        kernel,
        out_shape=(
            jax.ShapeDtypeStruct((NK, D), F32),
            jax.ShapeDtypeStruct((NC, D), F32),
            jax.ShapeDtypeStruct((PASSES, NP), F32),
        ),
        in_specs=[pl.BlockSpec(memory_space=pl.ANY)] * 5,
        out_specs=[pl.BlockSpec(memory_space=pltpu.VMEM)] * 3,
        scratch_shapes=scratch,
        compiler_params=pltpu.CompilerParams(
            collective_id=0, has_side_effects=True, vmem_limit_bytes=48 * 1024 * 1024
        ),
    )(points, fine_assign, fine_start, coarse_start, coarse_assign.reshape(1, NK)))


def solution(mesh):
    placed = (P("pts", None), P(None, "pts"), P("cen", None), P(), P("cen"))
    return jax.shard_map(
        on_device,
        mesh=mesh,
        in_specs=placed,
        out_specs=(P("cen", None), P(), P(None, "pts")),
        check_vma=False,
    )
```

time: 300 us -> 95.5 us (0.32)
  the two profiles are of different devices: /device:TPU:2 before, /device:TPU:1 now
where the time goes in v1:
time: 95.5 us; the launch traced here: 93.6 us
  Pallas kernels  87.5 us (92%)
  local copies, waits for them, and re-layouts  5.51 us (6%)
    pallas_call x1, Pallas kernels, on_device(): pl.pallas_call(kernel, out_shape=(jax.ShapeDtypeStruct((NK, D), F32), jax...  87.5 us
    unnamed x11, local copies, waits for them, and re-layouts  5.51 us

profile of v1, /device:TPU:1, one launch (start us, length us, event | category | flops | bytes accessed | tf_op | source)
XLA Modules:
  0.0 93.6 jit_solution(3109368877980805241)
XLA Ops:
  0.6 0.0 copy-start
  0.6 1.0 %copy-done = f32[128,1024]{1,0:T(8,128)S(1)} copy-done((f32[128,1024]{1,0:T(8,128)S(1)}, f32[128,1024]{1,0:T(8,128)}, u32[]{:S(2)}) %copy-start) | copy-done | bytes 524312
  1.7 0.0 copy-start.1
  1.7 0.9 %copy-done.1 = f32[64,1024]{1,0:T(8,128)S(1)} copy-done((f32[64,1024]{1,0:T(8,128)S(1)}, f32[64,1024]{1,0:T(8,128)}, u32[]{:S(2)}) %copy-start.1) | copy-done | bytes 262168
  2.6 0.0 copy-start.2
  2.6 0.8 copy-done.2
  3.4 0.0 copy-start.3
  3.4 0.7 copy-done.3
  4.0 87.5 %shard_map.76 = (f32[128,1024]{1,0:T(8,128)S(1)}, f32[64,1024]{1,0:T(8,128)S(1)}, f32[2,4096]{1,0:T(2,128)S(1)}) custom-call(bf16[4096,1024]{1,0:T(8,128)(2,1)} %points.1, s32[2,4096]{1,0:T(2,128)S(1)} %copy-done.2, f32[128,1024]{1,0:T(8,128)S(1)} %copy-done, f32[64,1024]{1,0:T(8,128)S(1)} %copy-done.1, s32[1,128]{1,0:T(1,128)S(1)} %bitcast.1), custom_call_target="tpu_custom_call" | custom-call | tf_op jit(solution)/shard_map/pallas_call | solution.py:337
  91.5 0.8 copy.11
  92.3 0.7 copy.12
  93.0 0.6 copy.13
Async XLA Ops:
  0.6 1.0 %copy-start = (f32[128,1024]{1,0:T(8,128)S(1)}, f32[128,1024]{1,0:T(8,128)}, u32[]{:S(2)}) copy-start(f32[128,1024]{1,0:T(8,128)} %fine_start.1) | copy-start | bytes 1572868
  1.7 0.9 %copy-start.1 = (f32[64,1024]{1,0:T(8,128)S(1)}, f32[64,1024]{1,0:T(8,128)}, u32[]{:S(2)}) copy-start(f32[64,1024]{1,0:T(8,128)} %coarse_start.1) | copy-start | bytes 786436
  2.6 0.8 copy-start.2
  3.4 0.7 copy-start.3

commit v2 on v1

--- a/solution.py
+++ b/solution.py
@@ -30,12 +30,12 @@
 
 def kernel(
     points, assign, fine_start, coarse_start, coarse_assign,
-    fine_out, coarse_out, gaps_out,
+    fine_hbm, coarse_hbm, gaps_hbm,
     xv, av, fv, cv, kv, in_sem,
-    low, norm, squares, wv, cacc,
+    low, norm, prods, squares, wv, cacc,
     ahead, hop_r, hop_l, blk_r, blk_l, got_l, got_r, ysend, yrecv,
     fine_g, cpack, crecv, coarse_g,
-    pn, pn_recv, gap_g,
+    pn, pn_recv, gap_g, fine_out, coarse_out, gaps_out, out_sem,
     rs_s, rs_r, ys_s, ys_r, gy_s, gy_r, gx_s, gx_r, cs_s, cs_r, cy_s, cy_r, cx_s, cx_r, p_s, p_r, g_s, g_r,
 ):
     pts = lax.axis_index("pts")
@@ -54,6 +54,11 @@
 
     sends = []
 
+    def arrive(name, *copies):
+        with jax.named_scope(name):
+            for copy in copies:
+                copy.wait_recv()
+
     def remote(src, dst, s, r, where):
         copy = pltpu.make_async_remote_copy(
             src_ref=src, dst_ref=dst, send_sem=s, recv_sem=r, device_id=where, device_id_type=MESH
@@ -69,46 +74,50 @@
         rows = pl.ds(pl.multiple_of(i * CH, CH), CH)
         return pltpu.make_async_copy(points.at[rows], xv.at[rows], in_sem.at[i])
 
-    for i in range(STEPS):
-        x_copy(i).start()
     a_in = pltpu.make_async_copy(assign, av, in_sem.at[STEPS + 1])
     k_in = pltpu.make_async_copy(coarse_assign, kv, in_sem.at[STEPS + 2])
     c_in = pltpu.make_async_copy(coarse_start, cv, in_sem.at[STEPS + 3])
     a_in.start()
     k_in.start()
     c_in.start()
+    for i in range(STEPS):
+        x_copy(i).start()
 
     barrier = pltpu.get_barrier_semaphore()
     for where in [right, left] + [y_peer(d) for d in range(1, NY)] + [c_peer(d) for d in range(1, NCEN)]:
         pl.semaphore_signal(barrier, inc=1, device_id=where, device_id_type=MESH)
 
-    fine_in.wait()
+    with jax.named_scope('w_fine_in'):
+        fine_in.wait()
     total = jnp.zeros((1, NK), F32)
     for b in range(D // 128):
         t = fv[:, b * 128 : (b + 1) * 128].T
         low[b * 128 : (b + 1) * 128, :] = t.astype(BF16)
         total = total + jnp.sum(t * t, axis=0, keepdims=True)
     norm[...] = total
-    a_in.wait()
-    k_in.wait()
-    c_in.wait()
+    with jax.named_scope('w_ins'):
+        a_in.wait()
+        k_in.wait()
+        c_in.wait()
 
     own = lax.broadcasted_iota(jnp.int32, (NK, CH), 0) + cen * NK
 
     def energies(p):
         cacc[...] = jnp.zeros_like(cacc)
 
-        def body(i, carry):
+        def multiply(i):
             if p == 0:
                 x_copy(i).wait()
             rows = pl.ds(pl.multiple_of(i * CH, CH), CH)
-            xs = xv[rows, :]
-            products = jnp.dot(xs, low[...], preferred_element_type=F32)
-            energy = (norm[...] - 2.0 * products).T
+            prods[i % 2] = jnp.dot(xv[rows, :], low[...], preferred_element_type=F32)
+
+        def select(i):
+            rows = pl.ds(pl.multiple_of(i * CH, CH), CH)
+            energy = (norm[...] - 2.0 * prods[i % 2]).T
             if p == 0:
                 part = jnp.zeros((CH, 128), F32)
                 for g in range(D // 128):
-                    xf = xs[:, g * 128 : (g + 1) * 128].astype(F32)
+                    xf = xv[rows, g * 128 : (g + 1) * 128].astype(F32)
                     part = part + xf * xf
                 sq = jnp.sum(part.T, axis=0, keepdims=True)
                 squares[i] = sq
@@ -127,9 +136,15 @@
             for g in range(CH // GP):
                 pn[i * (CH // GP) + g, 2 * p : 2 * p + 1, :] = picked[:, g * GP : (g + 1) * GP]
                 pn[i * (CH // GP) + g, 2 * p + 1 : 2 * p + 2, :] = nearest[:, g * GP : (g + 1) * GP]
+
+        def body(i, carry):
+            multiply(i + 1)
+            select(i)
             return carry
 
-        lax.fori_loop(0, STEPS, body, 0)
+        multiply(0)
+        lax.fori_loop(0, STEPS - 1, body, 0)
+        select(STEPS - 1)
 
     def block(b):
         cols = pl.multiple_of(b * 128, 128)
@@ -145,11 +160,10 @@
     pick_b = (of == kv[...] + NC).astype(F32)
     coarse = cpack[pl.ds(pl.multiple_of(share * 16, 16), 16), :]
 
-    pl.semaphore_wait(barrier, 2 + (NY - 1) + (NCEN - 1))
-
     for p in range(PASSES):
         last = p == PASSES - 1
-        energies(p)
+        with jax.named_scope(f'energies{p}'):
+            energies(p)
         if last:
             pn_copies = [
                 remote(pn.at[(cen + d) % NCEN], pn_recv.at[d], p_s.at[d], p_r.at[d], c_peer(d))
@@ -158,6 +172,9 @@
         counts8 = jnp.sum(cacc[...].T.reshape(16, 8, NK), axis=0)
 
         t = block(x_far)
+        if p == 0:
+            with jax.named_scope('w_barrier'):
+                pl.semaphore_wait(barrier, 2 + (NY - 1) + (NCEN - 1))
         ahead[p, 0:8, :] = counts8
         ahead[p, 8:ROWS, :] = t
         h1 = remote(ahead.at[p, 0:FIRST], hop_r.at[p], rs_s.at[p, 0], rs_r.at[p, 0], right)
@@ -173,17 +190,16 @@
         blk_l[p, 0:8, :] = counts8
         blk_l[p, 8:FIRST, :] = t[:128]
         l1 = remote(blk_l.at[p, 0:FIRST], got_r.at[p, 0:FIRST], rs_s.at[p, 3], rs_r.at[p, 3], left)
-        h1.wait_recv()
+        arrive('w_h1', h1)
         blk_r[p, 0:FIRST, :] += hop_r[p]
         r1 = remote(blk_r.at[p, 0:FIRST], got_l.at[p, 0:FIRST], rs_s.at[p, 4], rs_r.at[p, 4], right)
-        h2.wait_recv()
+        arrive('w_h2', h2)
         blk_l[p, FIRST:ROWS, :] = t[128:] + hop_l[p]
         l2 = remote(
             blk_l.at[p, FIRST:ROWS], got_r.at[p, FIRST:ROWS], rs_s.at[p, 5], rs_r.at[p, 5], left
         )
         t = block(x)
-        for copy in (r2, l1, r1, l2):
-            copy.wait_recv()
+        arrive('w_rsx', r2, l1, r1, l2)
         counts8 = counts8 + got_l[p, 0:8, :] + got_r[p, 0:8, :]
         t = t + got_l[p, 8:ROWS, :] + got_r[p, 8:ROWS, :]
         for k in range(NY):
@@ -206,8 +222,8 @@
         if last:
             finish = pn[cen]
             picked0, near0, picked1, near1 = (finish[k : k + 1] for k in range(4))
+            arrive('w_pn', *pn_copies)
             for d in range(1, NCEN):
-                pn_copies[d - 1].wait_recv()
                 picked0 = picked0 + pn_recv[d, 0:1, :]
                 near0 = jnp.minimum(near0, pn_recv[d, 1:2, :])
                 picked1 = picked1 + pn_recv[d, 2:3, :]
@@ -218,8 +234,8 @@
                 remote(gap_g.at[cen], gap_g.at[cen], g_s.at[d], g_r.at[d], c_peer(d)) for d in range(1, NCEN)
             ]
         all_sum = ysend[p, y]
+        arrive('w_rsy', *ycopies)
         for d in range(1, NY):
-            ycopies[d - 1].wait_recv()
             all_sum = all_sum + yrecv[p, d]
         counts = jnp.sum(all_sum[32:40], axis=0, keepdims=True)
         fine = (all_sum[0:32] + PRIOR * lookup) / (counts + PRIOR)
@@ -235,8 +251,7 @@
             remote(crecv.at[p, cen], crecv.at[p, cen], cs_s.at[p, d], cs_r.at[p, d], c_peer(d))
             for d in range(1, NCEN)
         ]
-        for copy in gy:
-            copy.wait_recv()
+        arrive('w_gy', *gy)
         lo, hi = pl.ds(0, NY // 2), pl.ds(NY // 2, NY // 2)
 
         def to(where, half, sem):
@@ -254,15 +269,14 @@
                 remote(coarse_g.at[x, y], coarse_g.at[x, y], cy_s.at[d], cy_r.at[d], y_peer(d))
                 for d in range(1, NY)
             ]
-        r_lo.wait_recv()
+        arrive('w_rlo', r_lo)
         ref = fine_g.at[p, x_left, lo]
         f_r = remote(ref, ref, gx_s.at[p, 4], gx_r.at[p, 4], right)
-        l_hi.wait_recv()
+        arrive('w_lhi', l_hi)
         ref = fine_g.at[p, x_right, hi]
         f_l = remote(ref, ref, gx_s.at[p, 5], gx_r.at[p, 5], left)
         if last:
-            for copy in cy:
-                copy.wait_recv()
+            arrive('w_cy', *cy)
 
             def coarse_to(where, half, sem):
                 ref = coarse_g.at[x, half]
@@ -272,17 +286,17 @@
             cl_hi = coarse_to(left, hi, 1)
             cr_hi = coarse_to(right, hi, 2)
             cl_lo = coarse_to(left, lo, 3)
-            for d in range(1, NCEN):
-                gap_copies[d - 1].wait_recv()
+            arrive('w_gap', *gap_copies)
             for c in range(NCEN):
                 gaps_out[:, c * GP : (c + 1) * GP] = gap_g[c]
-        for copy in (r_hi, l_lo, f_r, f_l):
-            copy.wait_recv()
-        if last:
-            cr_lo.wait_recv()
+            g_write = pltpu.make_async_copy(gaps_out, gaps_hbm, out_sem.at[2])
+            g_write.start()
+        arrive('w_gx', r_hi, l_lo, f_r, f_l)
+        if last:
+            arrive('w_crlo', cr_lo)
             ref = coarse_g.at[x_left, lo]
             cf_r = remote(ref, ref, cx_s.at[4], cx_r.at[4], right)
-            cl_hi.wait_recv()
+            arrive('w_clhi', cl_hi)
             ref = coarse_g.at[x_right, hi]
             cf_l = remote(ref, ref, cx_s.at[5], cx_r.at[5], left)
         total = jnp.zeros((1, NK), F32)
@@ -294,25 +308,46 @@
             else:
                 low[b * 128 : (b + 1) * 128, :] = t.astype(BF16)
                 total = total + jnp.sum(t * t, axis=0, keepdims=True)
-        if not last:
+        if last:
+            f_write = pltpu.make_async_copy(fine_out, fine_hbm, out_sem.at[0])
+            f_write.start()
+        else:
             norm[...] = total
 
-    for copy in (cr_hi, cl_lo, cf_r, cf_l):
-        copy.wait_recv()
+    arrive('w_cx', cr_hi, cl_lo, cf_r, cf_l)
     t = coarse_g[...].reshape(512, 128).T
     coarse_out[:, 0:512] = t[0:NC]
     coarse_out[:, 512:1024] = t[NC : 2 * NC]
-    for copy in sends:
-        copy.wait_send()
+    c_write = pltpu.make_async_copy(coarse_out, coarse_hbm, out_sem.at[1])
+    c_write.start()
+    with jax.named_scope('w_sends'):
+        for copy in sends:
+            copy.wait_send()
+    for copy in (g_write, f_write, c_write):
+        copy.wait()
 
 
 def coarse_update(copies, crecv, p, coarse):
-    for copy in copies:
-        copy.wait_recv()
+    with jax.named_scope('w_coarse'):
+        for copy in copies:
+            copy.wait_recv()
     total = crecv[p, 0]
     for c in range(1, NCEN):
         total = total + crecv[p, c]
     return (total[0:16] + PRIOR * coarse) / (total[16:17] + PRIOR)
+
+
+def write_out(fine, coarse, gaps, fine_hbm, coarse_hbm, gaps_hbm, fine_v, coarse_v, gaps_v, sem):
+    through = ((fine, fine_v, fine_hbm), (coarse, coarse_v, coarse_hbm), (gaps, gaps_v, gaps_hbm))
+    reads = [pltpu.make_async_copy(src, via, sem.at[0, i]) for i, (src, via, _) in enumerate(through)]
+    writes = [pltpu.make_async_copy(via, dst, sem.at[1, i]) for i, (_, via, dst) in enumerate(through)]
+    for copy in reads:
+        copy.start()
+    for read, write in zip(reads, writes):
+        read.wait()
+        write.start()
+    for copy in writes:
+        copy.wait()
 
 
 def on_device(points, fine_assign, fine_start, coarse_start, coarse_assign):
@@ -322,7 +357,7 @@
     scratch = [
         vmem((NP, D), BF16), vmem((PASSES, NP), jnp.int32), vmem((NK, D), F32), vmem((NC, D), F32),
         vmem((1, NK), jnp.int32), dma((STEPS + 4,)),
-        vmem((D, NK), BF16), vmem((1, NK), F32), vmem((STEPS, 1, CH), F32), vmem((2 * NK, NP), BF16),
+        vmem((D, NK), BF16), vmem((1, NK), F32), vmem((2, CH, NK), F32), vmem((STEPS, 1, CH), F32), vmem((2 * NK, NP), BF16),
         vmem((NK, 128), F32),
         vmem((n, ROWS, 128), F32), vmem((n, FIRST, 128), F32), vmem((n, 128, 128), F32),
         vmem((n, ROWS, 128), F32), vmem((n, ROWS, 128), F32), vmem((n, ROWS, 128), F32), vmem((n, ROWS, 128), F32),
@@ -330,24 +365,34 @@
         vmem((n, NX, NY, 32, 128), F32), vmem((512, 128), F32), vmem((n, NCEN, 24, 128), F32),
         vmem((NX, NY, 16, 128), F32),
         vmem((NCEN, 4, GP), F32), vmem((NCEN, 4, GP), F32), vmem((NCEN, 2, GP), F32),
+        vmem((NK, D), F32), vmem((NC, D), F32), vmem((PASSES, NP), F32), dma((3,)),
         dma((n, 6)), dma((n, 6)), dma((n, NY)), dma((n, NY)), dma((n, NY)), dma((n, NY)),
         dma((n, 6)), dma((n, 6)), dma((n, NCEN)), dma((n, NCEN)), dma((NY,)), dma((NY,)),
         dma((6,)), dma((6,)), dma((NCEN,)), dma((NCEN,)), dma((NCEN,)), dma((NCEN,)),
     ]
-    return tuple(pl.pallas_call(
+    shapes = (
+        jax.ShapeDtypeStruct((NK, D), F32),
+        jax.ShapeDtypeStruct((NC, D), F32),
+        jax.ShapeDtypeStruct((PASSES, NP), F32),
+    )
+    outs = pl.pallas_call(
         kernel,
-        out_shape=(
-            jax.ShapeDtypeStruct((NK, D), F32),
-            jax.ShapeDtypeStruct((NC, D), F32),
-            jax.ShapeDtypeStruct((PASSES, NP), F32),
-        ),
+        out_shape=shapes,
         in_specs=[pl.BlockSpec(memory_space=pl.ANY)] * 5,
-        out_specs=[pl.BlockSpec(memory_space=pltpu.VMEM)] * 3,
+        out_specs=[pl.BlockSpec(memory_space=pl.ANY)] * 3,
         scratch_shapes=scratch,
         compiler_params=pltpu.CompilerParams(
-            collective_id=0, has_side_effects=True, vmem_limit_bytes=48 * 1024 * 1024
+            collective_id=0, has_side_effects=True, vmem_limit_bytes=67043328
         ),
-    )(points, fine_assign, fine_start, coarse_start, coarse_assign.reshape(1, NK)))
+    )(points, fine_assign, fine_start, coarse_start, coarse_assign.reshape(1, NK))
+    return tuple(pl.pallas_call(
+        write_out,
+        out_shape=shapes,
+        in_specs=[pl.BlockSpec(memory_space=pl.ANY)] * 3,
+        out_specs=[pl.BlockSpec(memory_space=pl.ANY)] * 3,
+        scratch_shapes=[vmem((NK, D), F32), vmem((NC, D), F32), vmem((PASSES, NP), F32), dma((2, 3))],
+        compiler_params=pltpu.CompilerParams(vmem_limit_bytes=67043328),
+    )(*outs))
 
 
 def solution(mesh):

time: 95.5 us -> 90.9 us (0.952); the launches traced: 93.6 us -> 90 us
  local copies, waits for them, and re-layouts: 5.51 us -> 0 us
  Pallas kernels: 87.5 us -> 89.4 us
    unnamed x11 -> x0, local copies, waits for them, and re-layouts: 5.51 us -> none
    pallas_call x1 -> x2, Pallas kernels: 87.5 us -> 89.4 us  [the longest x1 87.4 us: on_device(): pl.pallas_call(kernel, out_shape=shapes, in_specs=[pl.BlockSpec(memory_sp...]
where the time goes in v2:
time: 90.9 us; the launch traced here: 90 us
  Pallas kernels  89.4 us (98%)
    pallas_call x1, Pallas kernels, on_device(): pl.pallas_call(kernel, out_shape=shapes, in_specs=[pl.BlockSpec(memory_sp...  87.4 us
    pallas_call x1, Pallas kernels, on_device(): pl.pallas_call(write_out, out_shape=shapes, in_specs=[pl.BlockSpec(memory...  1.97 us

profile of v2, /device:TPU:1, one launch (start us, length us, event | category | flops | bytes accessed | tf_op | source)
XLA Modules:
  0.0 90.0 jit_solution(12699165097712030713)
XLA Ops:
  0.6 87.4 %shard_map.76 = (f32[128,1024]{1,0:T(8,128)}, f32[64,1024]{1,0:T(8,128)}, f32[2,4096]{1,0:T(2,128)}) custom-call(bf16[4096,1024]{1,0:T(8,128)(2,1)} %points.1, s32[2,4096]{1,0:T(2,128)} %assign.1, f32[128,1024]{1,0:T(8,128)} %fine_start.1, f32[64,1024]{1,0:T(8,128)} %coarse_start.1, s32[1,128]{1,0:T(1,128)} %bitcast.1), custom_call_target="tpu_custom_call" | custom-call | tf_op jit(solution)/shard_map/pallas_call | solution.py:378
  88.0 2.0 %shard_map.77 = (f32[128,1024]{1,0:T(8,128)}, f32[64,1024]{1,0:T(8,128)}, f32[2,4096]{1,0:T(2,128)}) custom-call(f32[128,1024]{1,0:T(8,128)} %get-tuple-element.6.fine, f32[64,1024]{1,0:T(8,128)} %get-tuple-element.7.coarse, f32[2,4096]{1,0:T(2,128)} %get-tuple-element.8.gaps), custom_call_target="tpu_custom_call" | custom-call | tf_op jit(solution)/shard_map/pallas_call | solution.py:388

commit v3 on v2

v3 whole, which is shorter than its diff:
```python
import jax
import jax.numpy as jnp
from jax import lax
from jax.experimental import pallas as pl
from jax.experimental.pallas import tpu as pltpu
from jax.sharding import PartitionSpec as P

NC = 64
PASSES = 2
PRIOR = 4.0
D = 1024
NP = 4096
NK = 128
NX, NY, NZ, NCEN = 4, 8, 8, 16
CH = 512
STEPS = NP // CH
GP = NP // NCEN
F32 = jnp.float32
BF16 = jnp.bfloat16
MESH = pl.DeviceIdType.MESH
HIGH = lax.Precision.HIGHEST


def dot_nt(a, b):
    return lax.dot_general(a, b, (((1,), (1,)), ((), ())), precision=HIGH, preferred_element_type=F32)


def kernel(
    points, assign, fine_start, coarse_start, coarse_assign,
    fine_hbm, coarse_hbm, gaps_hbm,
    xv, av, fv, cv, kv, in_sem,
    low, norm, prod_a, prod_b, squares, wv, cacc,
    far, hop_r, hop_l, blk_r, blk_l, got_l, got_r, own_s, ysend, yrecv,
    cnt_s, cnt_x, cnt_m, cnt_y,
    fine_g, cpack, crecv, zsum, cpart, coarse_g,
    pn, pn_recv, gap_g, fine_out, coarse_out, gaps_out, out_sem,
    rs_s, rs_r, ys_s, ys_r, gy_s, gy_r, gx_s, gx_r, cs_s, cs_r, cy_s, cy_r, cx_s, cx_r, p_s, p_r, g_s, g_r,
    nx_s, nx_r, ny_s, ny_r, cp_s, cp_r,
):
    pts = lax.axis_index("pts")
    cen = lax.axis_index("cen")
    y = pts // NX
    x = pts % NX
    z = cen // 2
    x_right, x_left, x_far = (x + 1) % NX, (x + 3) % NX, (x + 2) % NX
    right = {"pts": y * NX + x_right}
    left = {"pts": y * NX + x_left}
    beyond = {"pts": y * NX + x_far}
    partner = {"cen": cen + 1 - 2 * (cen % 2)}

    def y_peer(d):
        return {"pts": ((y + d) % NY) * NX + x}

    def c_peer(d):
        return {"cen": (cen + d) % NCEN}

    sends = []

    def arrive(name, *copies):
        with jax.named_scope(name):
            for copy in copies:
                copy.wait_recv()

    def remote(src, dst, s, r, where):
        copy = pltpu.make_async_remote_copy(
            src_ref=src, dst_ref=dst, send_sem=s, recv_sem=r, device_id=where, device_id_type=MESH
        )
        copy.start()
        sends.append(copy)
        return copy

    fine_in = pltpu.make_async_copy(fine_start, fv, in_sem.at[STEPS])
    fine_in.start()

    def x_copy(i):
        rows = pl.ds(pl.multiple_of(i * CH, CH), CH)
        return pltpu.make_async_copy(points.at[rows], xv.at[rows], in_sem.at[i])

    a_in = pltpu.make_async_copy(assign, av, in_sem.at[STEPS + 1])
    k_in = pltpu.make_async_copy(coarse_assign, kv, in_sem.at[STEPS + 2])
    c_in = pltpu.make_async_copy(coarse_start, cv, in_sem.at[STEPS + 3])
    a_in.start()
    k_in.start()
    c_in.start()
    for i in range(STEPS):
        x_copy(i).start()

    barrier = pltpu.get_barrier_semaphore()
    for where in [right, left, beyond] + [y_peer(d) for d in range(1, NY)] + [c_peer(d) for d in range(1, NCEN)]:
        pl.semaphore_signal(barrier, inc=1, device_id=where, device_id_type=MESH)

    with jax.named_scope('w_fine_in'):
        fine_in.wait()
    total = jnp.zeros((1, NK), F32)
    for b in range(D // 128):
        t = fv[:, b * 128 : (b + 1) * 128].T
        low[b * 128 : (b + 1) * 128, :] = t.astype(BF16)
        total = total + jnp.sum(t * t, axis=0, keepdims=True)
    norm[...] = total
    with jax.named_scope('w_ins'):
        a_in.wait()
        k_in.wait()
        c_in.wait()

    own = lax.broadcasted_iota(jnp.int32, (NK, CH), 0) + cen * NK

    def energies(p):
        cacc[...] = jnp.zeros_like(cacc)

        def multiply(i, prod):
            if p == 0:
                x_copy(i).wait()
            rows = pl.ds(pl.multiple_of(i * CH, CH), CH)
            prod[...] = jnp.dot(xv[rows, :], low[...], preferred_element_type=F32)

        def select(i, prod):
            rows = pl.ds(pl.multiple_of(i * CH, CH), CH)
            energy = (norm[...] - 2.0 * prod[...]).T
            if p == 0:
                part = jnp.zeros((CH, 128), F32)
                for g in range(D // 128):
                    xf = xv[rows, g * 128 : (g + 1) * 128].astype(F32)
                    part = part + xf * xf
                sq = jnp.sum(part.T, axis=0, keepdims=True)
                squares[i] = sq
            else:
                sq = squares[i]
            member = av[p : p + 1, rows] == own
            picked = jnp.sum(jnp.where(member, energy, 0.0), axis=0, keepdims=True)
            nearest = jnp.min(energy, axis=0, keepdims=True)
            weights = 1.0 / (1.0 + (sq + picked) / D)
            wm = jnp.where(member, weights, 0.0)
            high = wm.astype(BF16)
            wv[0:NK, rows] = high
            wv[NK : 2 * NK, rows] = (wm - high.astype(F32)).astype(BF16)
            for g in range(CH // 128):
                cacc[...] += wm[:, g * 128 : (g + 1) * 128]
            for g in range(CH // GP):
                pn[i * (CH // GP) + g, 2 * p : 2 * p + 1, :] = picked[:, g * GP : (g + 1) * GP]
                pn[i * (CH // GP) + g, 2 * p + 1 : 2 * p + 2, :] = nearest[:, g * GP : (g + 1) * GP]

        def body(i, carry):
            multiply(2 * i + 1, prod_b)
            select(2 * i, prod_a)
            multiply(2 * i + 2, prod_a)
            select(2 * i + 1, prod_b)
            return carry

        multiply(0, prod_a)
        lax.fori_loop(0, STEPS // 2 - 1, body, 0)
        multiply(STEPS - 1, prod_b)
        select(STEPS - 2, prod_a)
        select(STEPS - 1, prod_b)

    def pair(first, second, h):
        cols = [pl.ds(pl.multiple_of(h * 512 + b * 128, 128), 128) for b in (first, second)]
        rhs = jnp.concatenate([xv[:, cols[0]], xv[:, cols[1]]], axis=1)
        both = jnp.dot(wv[...], rhs, preferred_element_type=F32)
        return (both[:NK] + both[NK:]).T

    share = x * NY + y
    turned = jnp.concatenate([cv[:, 0:512], cv[:, 512:1024]], axis=0).T
    cpack[...] = turned
    of = lax.broadcasted_iota(jnp.int32, (128, NK), 0)
    pick_a = (of == kv[...]).astype(F32)
    pick_b = (of == kv[...] + NC).astype(F32)
    coarse = cpack[pl.ds(pl.multiple_of(share * 16, 16), 16), :]

    for p in range(PASSES):
        last = p == PASSES - 1
        with jax.named_scope(f'energies{p}'):
            energies(p)
        picks = (pick_a, pick_b)
        cnt = jnp.sum(cacc[...].T, axis=0, keepdims=True)
        cnt_s[p] = cnt
        LO, HI = pl.ds(0, 64), pl.ds(64, 64)

        hops = []
        for h in range(2):
            t = pair(x_far, x_right, h)
            far[p, h] = t[:128]
            blk_r[p, h] = t[128:]
            if p == 0 and h == 0:
                with jax.named_scope('w_barrier'):
                    pl.semaphore_wait(barrier, 3 + (NY - 1) + (NCEN - 1))
            to_r = remote(far.at[p, h, LO], hop_r.at[p, h], rs_s.at[p, h, 0], rs_r.at[p, h, 0], right)
            to_l = remote(far.at[p, h, HI], hop_l.at[p, h], rs_s.at[p, h, 1], rs_r.at[p, h, 1], left)
            r2 = remote(blk_r.at[p, h, HI], got_l.at[p, h, HI], rs_s.at[p, h, 2], rs_r.at[p, h, 2], right)
            if h == 0:
                ncopies = [
                    remote(cnt_s.at[p], cnt_x.at[p, k], nx_s.at[p, k], nx_r.at[p, k], where)
                    for k, where in enumerate((right, left, beyond))
                ]
            t = pair(x_left, x, h)
            blk_l[p, h] = t[:128]
            own_s[h] = t[128:]
            l1 = remote(blk_l.at[p, h, LO], got_r.at[p, h, LO], rs_s.at[p, h, 3], rs_r.at[p, h, 3], left)
            hops.append((to_r, to_l, r2, l1))
        if last:
            pn_copies = [
                remote(pn.at[(cen + d) % NCEN], pn_recv.at[d], p_s.at[d], p_r.at[d], c_peer(d))
                for d in range(1, NCEN)
            ]
        waits = []
        for h in range(2):
            to_r, to_l, r2, l1 = hops[h]
            arrive(f'w_hop{h}', to_r)
            blk_r[p, h, 0:64, :] += hop_r[p, h]
            r1 = remote(blk_r.at[p, h, LO], got_l.at[p, h, LO], rs_s.at[p, h, 4], rs_r.at[p, h, 4], right)
            arrive(f'w_hop{h}', to_l)
            blk_l[p, h, 64:128, :] += hop_l[p, h]
            l2 = remote(blk_l.at[p, h, HI], got_r.at[p, h, HI], rs_s.at[p, h, 5], rs_r.at[p, h, 5], left)
            waits.append((r2, l1, r1, l2))
        arrive('w_nx', *ncopies)
        cnt = cnt + cnt_x[p, 0] + cnt_x[p, 1] + cnt_x[p, 2]
        cnt_m[p] = cnt
        mcopies = [
            remote(cnt_m.at[p], cnt_y.at[p, d], ny_s.at[p, d], ny_r.at[p, d], y_peer(d)) for d in range(1, NY)
        ]
        ycopies = []
        for h in range(2):
            arrive(f'w_rsx{h}', *waits[h])
            ysend[p, h] = (own_s[h] + got_l[p, h] + got_r[p, h]).reshape(NY, 16, 128)
            ycopies.append([
                remote(
                    ysend.at[p, h, (y + d) % NY], yrecv.at[p, h, d], ys_s.at[p, h, d], ys_r.at[p, h, d], y_peer(d)
                )
                for d in range(1, NY)
            ])
        if p > 0:
            coarse = coarse_update([pcopy], zsum, cpart, p - 1, coarse)
        lookups = [jnp.dot(coarse, pick, precision=HIGH, preferred_element_type=F32) for pick in picks]
        if last:
            finish = pn[cen]
            picked0, near0, picked1, near1 = (finish[k : k + 1] for k in range(4))
            arrive('w_pn', *pn_copies)
            for d in range(1, NCEN):
                picked0 = picked0 + pn_recv[d, 0:1, :]
                near0 = jnp.minimum(near0, pn_recv[d, 1:2, :])
                picked1 = picked1 + pn_recv[d, 2:3, :]
                near1 = jnp.minimum(near1, pn_recv[d, 3:4, :])
            gap_g[cen, 0:1, :] = (picked0 - near0) / 32.0
            gap_g[cen, 1:2, :] = (picked1 - near1) / 32.0
            gap_copies = [
                remote(gap_g.at[cen], gap_g.at[cen], g_s.at[d], g_r.at[d], c_peer(d)) for d in range(1, NCEN)
            ]
        arrive('w_ny', *mcopies)
        counts = cnt
        for d in range(1, NY):
            counts = counts + cnt_y[p, d]
        part = None
        gy = []
        for h in range(2):
            arrive(f'w_rsy{h}', *ycopies[h])
            total = ysend[p, h, y]
            for d in range(1, NY):
                total = total + yrecv[p, h, d]
            fine = (total + PRIOR * lookups[h]) / (counts + PRIOR)
            fine_g[p, h, x, y] = fine
            ref = fine_g.at[p, h, x, y]
            gy.append([remote(ref, ref, gy_s.at[p, h, d], gy_r.at[p, h, d], y_peer(d)) for d in range(1, NY)])
            weighted = dot_nt(counts * fine, picks[h])
            part = weighted if part is None else part + weighted
        crecv[p, z, 0:16, :] = part
        crecv[p, z, 16:24, :] = dot_nt(jnp.broadcast_to(counts, (8, NK)), pick_a + pick_b)
        ccopies = [
            remote(crecv.at[p, z], crecv.at[p, z], cs_s.at[p, d], cs_r.at[p, d], c_peer(2 * d))
            for d in range(1, NZ)
        ]
        lo, hi = pl.ds(0, NY // 2), pl.ds(NY // 2, NY // 2)
        firsts = []
        for h in range(2):
            arrive(f'w_gy{h}', *gy[h])

            def to(where, half, sem, h=h):
                ref = fine_g.at[p, h, x, half]
                return remote(ref, ref, gx_s.at[p, h, sem], gx_r.at[p, h, sem], where)

            firsts.append((to(right, lo, 0), to(left, hi, 1), to(right, hi, 2), to(left, lo, 3)))
        ends = []

        def forward(h):
            r_lo, l_hi, r_hi, l_lo = firsts[h]
            arrive(f'w_gx{h}', r_lo)
            ref = fine_g.at[p, h, x_left, lo]
            f_r = remote(ref, ref, gx_s.at[p, h, 4], gx_r.at[p, h, 4], right)
            arrive(f'w_gx{h}', l_hi)
            ref = fine_g.at[p, h, x_right, hi]
            f_l = remote(ref, ref, gx_s.at[p, h, 5], gx_r.at[p, h, 5], left)
            ends.extend((r_hi, l_lo, f_r, f_l))

        def chip_sum():
            arrive('w_cz', *ccopies)
            total = crecv[p, 0]
            for c in range(1, NZ):
                total = total + crecv[p, c]
            zsum[p] = total
            return remote(zsum.at[p], cpart.at[p], cp_s.at[p], cp_r.at[p], partner)

        if not last:
            forward(0)
            forward(1)
            pcopy = chip_sum()
        else:
            forward(0)
            pcopy = chip_sum()
            forward(1)
            coarse = coarse_update([pcopy], zsum, cpart, p, coarse)
            coarse_g[x, y] = coarse
            cy = [
                remote(coarse_g.at[x, y], coarse_g.at[x, y], cy_s.at[d], cy_r.at[d], y_peer(d))
                for d in range(1, NY)
            ]
            arrive('w_gap', *gap_copies)
            for c in range(NCEN):
                gaps_out[:, c * GP : (c + 1) * GP] = gap_g[c]
            g_write = pltpu.make_async_copy(gaps_out, gaps_hbm, out_sem.at[2])
            g_write.start()
            arrive('w_cy', *cy)

            def coarse_to(where, half, sem):
                ref = coarse_g.at[x, half]
                return remote(ref, ref, cx_s.at[sem], cx_r.at[sem], where)

            cr_lo = coarse_to(right, lo, 0)
            cl_hi = coarse_to(left, hi, 1)
            cr_hi = coarse_to(right, hi, 2)
            cl_lo = coarse_to(left, lo, 3)
        arrive('w_gx', *ends)
        total = jnp.zeros((1, NK), F32)
        for b in range(D // 128):
            h, bx = divmod(b, NX)
            t = fine_g[p, h, bx].reshape(128, NK)
            if last:
                fine_out[:, b * 128 : (b + 1) * 128] = t.T
            else:
                low[b * 128 : (b + 1) * 128, :] = t.astype(BF16)
                total = total + jnp.sum(t * t, axis=0, keepdims=True)
        if last:
            f_write = pltpu.make_async_copy(fine_out, fine_hbm, out_sem.at[0])
            f_write.start()
            arrive('w_crlo', cr_lo)
            ref = coarse_g.at[x_left, lo]
            cf_r = remote(ref, ref, cx_s.at[4], cx_r.at[4], right)
            arrive('w_clhi', cl_hi)
            ref = coarse_g.at[x_right, hi]
            cf_l = remote(ref, ref, cx_s.at[5], cx_r.at[5], left)
        else:
            norm[...] = total

    arrive('w_cx', cr_hi, cl_lo, cf_r, cf_l)
    t = coarse_g[...].reshape(512, 128).T
    coarse_out[:, 0:512] = t[0:NC]
    coarse_out[:, 512:1024] = t[NC : 2 * NC]
    c_write = pltpu.make_async_copy(coarse_out, coarse_hbm, out_sem.at[1])
    c_write.start()
    with jax.named_scope('w_sends'):
        for copy in sends:
            copy.wait_send()
    for copy in (g_write, f_write, c_write):
        copy.wait()


def coarse_update(copies, zsum, cpart, p, coarse):
    with jax.named_scope('w_coarse'):
        for copy in copies:
            copy.wait_recv()
    total = zsum[p] + cpart[p]
    return (total[0:16] + PRIOR * coarse) / (total[16:17] + PRIOR)


def write_out(fine, coarse, gaps, fine_hbm, coarse_hbm, gaps_hbm, fine_v, coarse_v, gaps_v, sem):
    through = ((fine, fine_v, fine_hbm), (coarse, coarse_v, coarse_hbm), (gaps, gaps_v, gaps_hbm))
    reads = [pltpu.make_async_copy(src, via, sem.at[0, i]) for i, (src, via, _) in enumerate(through)]
    writes = [pltpu.make_async_copy(via, dst, sem.at[1, i]) for i, (_, via, dst) in enumerate(through)]
    for copy in reads:
        copy.start()
    for read, write in zip(reads, writes):
        read.wait()
        write.start()
    for copy in writes:
        copy.wait()


def on_device(points, fine_assign, fine_start, coarse_start, coarse_assign):
    dma = pltpu.SemaphoreType.DMA
    vmem = pltpu.VMEM
    n = PASSES
    scratch = [
        vmem((NP, D), BF16), vmem((PASSES, NP), jnp.int32), vmem((NK, D), F32), vmem((NC, D), F32),
        vmem((1, NK), jnp.int32), dma((STEPS + 4,)),
        vmem((D, NK), BF16), vmem((1, NK), F32), vmem((CH, NK), F32), vmem((CH, NK), F32),
        vmem((STEPS, 1, CH), F32), vmem((2 * NK, NP), BF16), vmem((NK, 128), F32),
        vmem((n, 2, 128, 128), F32), vmem((n, 2, 64, 128), F32), vmem((n, 2, 64, 128), F32),
        vmem((n, 2, 128, 128), F32), vmem((n, 2, 128, 128), F32), vmem((n, 2, 128, 128), F32),
        vmem((n, 2, 128, 128), F32), vmem((2, 128, 128), F32),
        vmem((n, 2, NY, 16, 128), F32), vmem((n, 2, NY, 16, 128), F32),
        vmem((n, 1, 128), F32), vmem((n, 3, 1, 128), F32), vmem((n, 1, 128), F32), vmem((n, NY, 1, 128), F32),
        vmem((n, 2, NX, NY, 16, 128), F32), vmem((512, 128), F32), vmem((n, NZ, 24, 128), F32),
        vmem((n, 24, 128), F32), vmem((n, 24, 128), F32), vmem((NX, NY, 16, 128), F32),
        vmem((NCEN, 4, GP), F32), vmem((NCEN, 4, GP), F32), vmem((NCEN, 2, GP), F32),
        vmem((NK, D), F32), vmem((NC, D), F32), vmem((PASSES, NP), F32), dma((3,)),
        dma((n, 2, 6)), dma((n, 2, 6)), dma((n, 2, NY)), dma((n, 2, NY)), dma((n, 2, NY)), dma((n, 2, NY)),
        dma((n, 2, 6)), dma((n, 2, 6)), dma((n, NZ)), dma((n, NZ)), dma((NY,)), dma((NY,)),
        dma((6,)), dma((6,)), dma((NCEN,)), dma((NCEN,)), dma((NCEN,)), dma((NCEN,)),
        dma((n, 3)), dma((n, 3)), dma((n, NY)), dma((n, NY)), dma((n,)), dma((n,)),
    ]
    shapes = (
        jax.ShapeDtypeStruct((NK, D), F32),
        jax.ShapeDtypeStruct((NC, D), F32),
        jax.ShapeDtypeStruct((PASSES, NP), F32),
    )
    outs = pl.pallas_call(
        kernel,
        out_shape=shapes,
        in_specs=[pl.BlockSpec(memory_space=pl.ANY)] * 5,
        out_specs=[pl.BlockSpec(memory_space=pl.ANY)] * 3,
        scratch_shapes=scratch,
        compiler_params=pltpu.CompilerParams(
            collective_id=0, has_side_effects=True, vmem_limit_bytes=67043328
        ),
    )(points, fine_assign, fine_start, coarse_start, coarse_assign.reshape(1, NK))
    return tuple(pl.pallas_call(
        write_out,
        out_shape=shapes,
        in_specs=[pl.BlockSpec(memory_space=pl.ANY)] * 3,
        out_specs=[pl.BlockSpec(memory_space=pl.ANY)] * 3,
        scratch_shapes=[vmem((NK, D), F32), vmem((NC, D), F32), vmem((PASSES, NP), F32), dma((2, 3))],
        compiler_params=pltpu.CompilerParams(vmem_limit_bytes=67043328),
    )(*outs))


def solution(mesh):
    placed = (P("pts", None), P(None, "pts"), P("cen", None), P(), P("cen"))
    return jax.shard_map(
        on_device,
        mesh=mesh,
        in_specs=placed,
        out_specs=(P("cen", None), P(), P(None, "pts")),
        check_vma=False,
    )
```

time: 90.9 us -> 88.8 us (0.977)
  Pallas kernels: 89.4 us -> 87 us
    pallas_call x1, Pallas kernels: 87.4 us -> 85 us  [on_device(): pl.pallas_call(kernel, out_shape=shapes, in_specs=[pl.BlockSpec(memory_sp...]
where the time goes in v3:
time: 88.8 us; the launch traced here: 87.8 us
  Pallas kernels  87 us (98%)
    pallas_call x1, Pallas kernels, on_device(): pl.pallas_call(kernel, out_shape=shapes, in_specs=[pl.BlockSpec(memory_sp...  85 us
    pallas_call x1, Pallas kernels, on_device(): pl.pallas_call(write_out, out_shape=shapes, in_specs=[pl.BlockSpec(memory...  1.97 us

profile of v3, /device:TPU:1, one launch (start us, length us, event | category | flops | bytes accessed | tf_op | source)
XLA Modules:
  0.0 87.8 jit_solution(11537349298186278095)
XLA Ops:
  0.6 85.0 %shard_map.76 = (f32[128,1024]{1,0:T(8,128)}, f32[64,1024]{1,0:T(8,128)}, f32[2,4096]{1,0:T(2,128)}) custom-call(bf16[4096,1024]{1,0:T(8,128)(2,1)} %points.1, s32[2,4096]{1,0:T(2,128)} %assign.1, f32[128,1024]{1,0:T(8,128)} %fine_start.1, f32[64,1024]{1,0:T(8,128)} %coarse_start.1, s32[1,128]{1,0:T(1,128)} %bitcast.1), custom_call_target="tpu_custom_call" | custom-call | tf_op jit(solution)/shard_map/pallas_call | solution.py:413
  85.6 2.0 %shard_map.77 = (f32[128,1024]{1,0:T(8,128)}, f32[64,1024]{1,0:T(8,128)}, f32[2,4096]{1,0:T(2,128)}) custom-call(f32[128,1024]{1,0:T(8,128)} %get-tuple-element.6.fine, f32[64,1024]{1,0:T(8,128)} %get-tuple-element.7.coarse, f32[2,4096]{1,0:T(2,128)} %get-tuple-element.8.gaps), custom_call_target="tpu_custom_call" | custom-call | tf_op jit(solution)/shard_map/pallas_call | solution.py:423

commit v4 on v3

v4 whole, which is shorter than its diff:
```python
import jax
import jax.numpy as jnp
from jax import lax
from jax.experimental import pallas as pl
from jax.experimental.pallas import tpu as pltpu
from jax.sharding import PartitionSpec as P

NC = 64
PASSES = 2
PRIOR = 4.0
D = 1024
NP = 4096
NK = 128
NX, NY, NCEN = 4, 8, 16
CH = 512
STEPS = NP // CH
GP = NP // NCEN
F32 = jnp.float32
BF16 = jnp.bfloat16
MESH = pl.DeviceIdType.MESH
HIGH = lax.Precision.HIGHEST


def dot_nt(a, b):
    return lax.dot_general(a, b, (((1,), (1,)), ((), ())), precision=HIGH, preferred_element_type=F32)


def kernel(
    points, assign, fine_start, coarse_start, coarse_assign,
    fine_hbm, coarse_hbm, gaps_hbm,
    xv, av, fv, cv, kv, in_sem,
    low, norm, prod_a, prod_b, squares, wv, cacc,
    far, hop_r, hop_l, blk_r, blk_l, got_l, got_r, own_s, ysend, yrecv,
    cnt_s, cnt_x, cnt_m, cnt_y,
    fine_g, cpack, crecv, ccnt, halves, coarse_g,
    pn, pn_recv, gap_g, fine_out, coarse_out, gaps_out, out_sem,
    rs_s, rs_r, ys_s, ys_r, gy_s, gy_r, gx_s, gx_r, cs_s, cs_r, cn_s, cn_r, nx_s, nx_r, ny_s, ny_r,
    cy_s, cy_r, cx_s, cx_r, p_s, p_r, g_s, g_r, cp_s, cp_r,
):
    pts = lax.axis_index("pts")
    cen = lax.axis_index("cen")
    y = pts // NX
    x = pts % NX
    core = cen % 2
    x_right, x_left, x_far = (x + 1) % NX, (x + 3) % NX, (x + 2) % NX
    right = {"pts": y * NX + x_right}
    left = {"pts": y * NX + x_left}
    beyond = {"pts": y * NX + x_far}
    partner = {"cen": cen + 1 - 2 * core}

    def y_peer(d):
        return {"pts": ((y + d) % NY) * NX + x}

    def c_peer(d):
        return {"cen": (cen + d) % NCEN}

    sent = []

    def remote(src, dst, s, r, where):
        copy = pltpu.make_async_remote_copy(
            src_ref=src, dst_ref=dst, send_sem=s, recv_sem=r, device_id=where, device_id_type=MESH
        )
        copy.start()

    def waiter(ref, sem):
        return pltpu.make_async_remote_copy(
            src_ref=ref, dst_ref=ref, send_sem=sem, recv_sem=sem, device_id=right, device_id_type=MESH
        )

    def arrive(name, ref, sem):
        with jax.named_scope(name):
            waiter(ref, sem).wait_recv()

    def to_send(ref, sem):
        sent.append(waiter(ref, sem))

    fine_in = pltpu.make_async_copy(fine_start, fv, in_sem.at[STEPS])
    fine_in.start()

    def x_copy(i):
        rows = pl.ds(pl.multiple_of(i * CH, CH), CH)
        return pltpu.make_async_copy(points.at[rows], xv.at[rows, pl.ds(0, D)], in_sem.at[i])

    a_in = pltpu.make_async_copy(assign, av, in_sem.at[STEPS + 1])
    k_in = pltpu.make_async_copy(coarse_assign, kv, in_sem.at[STEPS + 2])
    c_in = pltpu.make_async_copy(coarse_start, cv, in_sem.at[STEPS + 3])
    a_in.start()
    k_in.start()
    c_in.start()
    for i in range(STEPS):
        x_copy(i).start()

    barrier = pltpu.get_barrier_semaphore()
    for where in [right, left, beyond] + [y_peer(d) for d in range(1, NY)] + [c_peer(d) for d in range(1, NCEN)]:
        pl.semaphore_signal(barrier, inc=1, device_id=where, device_id_type=MESH)

    with jax.named_scope('w_fine_in'):
        fine_in.wait()
    total = jnp.zeros((1, NK), F32)
    for b in range(D // 128):
        t = fv[:, b * 128 : (b + 1) * 128].T
        low[b * 128 : (b + 1) * 128, :] = t.astype(BF16)
        total = total + jnp.sum(t * t, axis=0, keepdims=True)
    norm[...] = total
    with jax.named_scope('w_ins'):
        a_in.wait()
        k_in.wait()
        c_in.wait()

    own = lax.broadcasted_iota(jnp.int32, (NK, 128), 0) + cen * NK

    def energies(p):
        cacc[...] = jnp.zeros_like(cacc)

        def multiply(i, prod):
            if p == 0:
                x_copy(i).wait()
            rows = pl.ds(pl.multiple_of(i * CH, CH), CH)
            prod[...] = jnp.dot(xv[rows, 0:D], low[...], preferred_element_type=F32)

        def select(i, prod):
            for g in range(CH // 128):
                here = slice(g * 128, (g + 1) * 128)
                rows = pl.ds(pl.multiple_of(i * CH + g * 128, 128), 128)
                energy = (norm[...] - 2.0 * prod[here, :]).T
                if p == 0:
                    part = jnp.zeros((128, 128), F32)
                    for f in range(D // 128):
                        xf = xv[rows, f * 128 : (f + 1) * 128].astype(F32)
                        part = part + xf * xf
                    sq = jnp.sum(part.T, axis=0, keepdims=True)
                    squares[i, :, here] = sq
                else:
                    sq = squares[i, :, here]
                member = av[p : p + 1, rows] == own
                picked = jnp.sum(jnp.where(member, energy, 0.0), axis=0, keepdims=True)
                nearest = jnp.min(energy, axis=0, keepdims=True)
                weights = 1.0 / (1.0 + (sq + picked) / D)
                wm = jnp.where(member, weights, 0.0)
                high = wm.astype(BF16)
                wv[0:NK, rows] = high
                wv[NK : 2 * NK, rows] = (wm - high.astype(F32)).astype(BF16)
                cacc[...] += wm
                at = i * (CH // GP) + g * 128 // GP
                lane = slice(g * 128 % GP, g * 128 % GP + 128)
                pn[at, 2 * p : 2 * p + 1, lane] = picked
                pn[at, 2 * p + 1 : 2 * p + 2, lane] = nearest

        def body(i, carry):
            multiply(2 * i + 1, prod_b)
            select(2 * i, prod_a)
            multiply(2 * i + 2, prod_a)
            select(2 * i + 1, prod_b)
            return carry

        multiply(0, prod_a)
        lax.fori_loop(0, STEPS // 2 - 1, body, 0)
        multiply(STEPS - 1, prod_b)
        select(STEPS - 2, prod_a)
        select(STEPS - 1, prod_b)

    def pair(first, second, h):
        cols = [pl.ds(pl.multiple_of(h * 512 + b * 128, 128), 128) for b in (first, second)]
        rhs = jnp.concatenate([xv[:, cols[0]], xv[:, cols[1]]], axis=1)
        both = jnp.dot(wv[:, 0:NP], rhs, preferred_element_type=F32)
        return (both[:NK] + both[NK:]).T

    share = x * NY + y
    turned = jnp.concatenate([cv[:, 0:512], cv[:, 512:1024]], axis=0).T
    cpack[...] = turned
    of = lax.broadcasted_iota(jnp.int32, (128, NK), 0)
    pick_a = (of == kv[...]).astype(F32)
    pick_b = (of == kv[...] + NC).astype(F32)
    coarse = cpack[pl.ds(pl.multiple_of(share * 16, 16), 16), :]

    for p in range(PASSES):
        last = p == PASSES - 1
        with jax.named_scope(f'energies{p}'):
            energies(p)
        picks = (pick_a, pick_b)
        cnt = jnp.sum(cacc[...].T, axis=0, keepdims=True)
        cnt_s[p] = cnt
        LO, HI = pl.ds(0, 64), pl.ds(64, 64)

        for h in range(2):
            ss, rr = rs_s.at[p, h], rs_r.at[p, h, 2]
            t = pair(x_far, x_right, h)
            far[p, h] = t[:128]
            blk_r[p, h] = t[128:]
            if p == 0 and h == 0:
                with jax.named_scope('w_barrier'):
                    pl.semaphore_wait(barrier, 3 + (NY - 1) + (NCEN - 1))
            remote(far.at[p, h, LO], hop_r.at[p, h], ss, rs_r.at[p, h, 0], right)
            remote(far.at[p, h, HI], hop_l.at[p, h], ss, rs_r.at[p, h, 1], left)
            remote(blk_r.at[p, h, HI], got_l.at[p, h, HI], ss, rr, right)
            if h == 0:
                for k, where in enumerate((right, left, beyond)):
                    remote(cnt_s.at[p], cnt_x.at[p, k], nx_s.at[p], nx_r.at[p], where)
                to_send(cnt_x.at[p], nx_s.at[p])
            t = pair(x_left, x, h)
            blk_l[p, h] = t[:128]
            own_s[h] = t[128:]
            remote(blk_l.at[p, h, LO], got_r.at[p, h, LO], ss, rr, left)
        if last:
            for d in range(1, NCEN):
                remote(pn.at[(cen + d) % NCEN], pn_recv.at[d], p_s.at[0], p_r.at[0], c_peer(d))
            to_send(pn_recv.at[pl.ds(1, NCEN - 1)], p_s.at[0])
        for h in range(2):
            ss, rr = rs_s.at[p, h], rs_r.at[p, h, 2]
            arrive(f'w_hop{h}', hop_r.at[p, h], rs_r.at[p, h, 0])
            blk_r[p, h, 0:64, :] += hop_r[p, h]
            remote(blk_r.at[p, h, LO], got_l.at[p, h, LO], ss, rr, right)
            arrive(f'w_hop{h}', hop_l.at[p, h], rs_r.at[p, h, 1])
            blk_l[p, h, 64:128, :] += hop_l[p, h]
            remote(blk_l.at[p, h, HI], got_r.at[p, h, HI], ss, rr, left)
            to_send(fine_g.at[p, h, pl.ds(0, 3)], ss)
        arrive('w_nx', cnt_x.at[p], nx_r.at[p])
        cnt = cnt + cnt_x[p, 0] + cnt_x[p, 1] + cnt_x[p, 2]
        cnt_m[p] = cnt
        for d in range(1, NY):
            remote(cnt_m.at[p], cnt_y.at[p, d], ny_s.at[p], ny_r.at[p], y_peer(d))
        others = pl.ds(1, NY - 1)
        to_send(cnt_y.at[p, others], ny_s.at[p])
        for h in range(2):
            arrive(f'w_rsx{h}', fine_g.at[p, h, pl.ds(0, 2)], rs_r.at[p, h, 2])
            ysend[p, h] = (own_s[h] + got_l[p, h] + got_r[p, h]).reshape(NY, 16, 128)
            for d in range(1, NY):
                remote(
                    ysend.at[p, h, (y + d) % NY], yrecv.at[p, h, d], ys_s.at[p, h], ys_r.at[p, h], y_peer(d)
                )
            to_send(yrecv.at[p, h, others], ys_s.at[p, h])
        if p > 0:
            arrive('w_coarse', crecv.at[p - 1, pl.ds(1, NCEN - 1)], cs_r.at[p - 1])
            arrive('w_coarse', ccnt.at[p - 1, pl.ds(1, NCEN - 1)], cn_r.at[p - 1])
            coarse = coarse_update(crecv[p - 1], ccnt[p - 1], coarse)
        lookups = [jnp.dot(coarse, pick, precision=HIGH, preferred_element_type=F32) for pick in picks]
        arrive('w_ny', cnt_y.at[p, others], ny_r.at[p])
        counts = cnt
        for d in range(1, NY):
            counts = counts + cnt_y[p, d]
        ccnt[p, cen] = dot_nt(jnp.broadcast_to(counts, (8, NK)), pick_a + pick_b)[0:1]
        for d in range(1, NCEN):
            remote(ccnt.at[p, cen], ccnt.at[p, cen], cn_s.at[p], cn_r.at[p], c_peer(d))
        to_send(ccnt.at[p, pl.ds(1, NCEN - 1)], cn_s.at[p])
        part = None
        for h in range(2):
            arrive(f'w_rsy{h}', yrecv.at[p, h, others], ys_r.at[p, h])
            total = ysend[p, h, y]
            for d in range(1, NY):
                total = total + yrecv[p, h, d]
            fine = (total + PRIOR * lookups[h]) / (counts + PRIOR)
            fine_g[p, h, x, y] = fine
            ref = fine_g.at[p, h, x, y]
            for d in range(1, NY):
                remote(ref, ref, gy_s.at[p, h], gy_r.at[p, h], y_peer(d))
            to_send(yrecv.at[p, h, others], gy_s.at[p, h])
            weighted = dot_nt(counts * fine, picks[h])
            part = weighted if part is None else part + weighted
        if last:
            mine = pl.ds(pl.multiple_of(core * 8, 8), 8)
            halves[0] = part
            halves[1] = coarse
            crecv[p, cen, 0:8, :] = halves[0, mine, :]
            for d in range(1, NCEN):
                theirs = pl.ds(pl.multiple_of((cen + d) % 2 * 8, 8), 8)
                remote(
                    halves.at[0, theirs], crecv.at[p, cen, pl.ds(0, 8)], cs_s.at[p], cs_r.at[p], c_peer(d)
                )
            some = crecv.at[p, pl.ds(1, NCEN - 1), pl.ds(0, 8)]
        else:
            crecv[p, cen] = part
            for d in range(1, NCEN):
                remote(crecv.at[p, cen], crecv.at[p, cen], cs_s.at[p], cs_r.at[p], c_peer(d))
            some = crecv.at[p, pl.ds(1, NCEN - 1)]
        to_send(some, cs_s.at[p])
        lo, hi = pl.ds(0, NY // 2), pl.ds(NY // 2, NY // 2)
        for h in range(2):
            arrive(f'w_gy{h}', yrecv.at[p, h, others], gy_r.at[p, h])
            low_half, high_half = fine_g.at[p, h, x, lo], fine_g.at[p, h, x, hi]
            ss = gx_s.at[p, h]
            remote(low_half, low_half, ss, gx_r.at[p, h, 0], right)
            remote(high_half, high_half, ss, gx_r.at[p, h, 1], left)
            remote(high_half, high_half, ss, gx_r.at[p, h, 2], right)
            remote(low_half, low_half, ss, gx_r.at[p, h, 2], left)

        def forward(h):
            ss, rr = gx_s.at[p, h], gx_r.at[p, h, 2]
            ref = fine_g.at[p, h, x_left, lo]
            arrive(f'w_gx{h}', ref, gx_r.at[p, h, 0])
            remote(ref, ref, ss, rr, right)
            ref = fine_g.at[p, h, x_right, hi]
            arrive(f'w_gx{h}', ref, gx_r.at[p, h, 1])
            remote(ref, ref, ss, rr, left)
            to_send(fine_g.at[p, h, pl.ds(0, 3)], ss)

        forward(0)
        if last:
            arrive('w_coarse', some, cs_r.at[p])
            arrive('w_coarse', ccnt.at[p, pl.ds(1, NCEN - 1)], cn_r.at[p])
            coarse_g[core, x, y] = coarse_update(crecv[p, :, 0:8, :], ccnt[p], halves[1, mine, :])
            ref = coarse_g.at[core, x, y]
            for d in range(1, NY):
                remote(ref, ref, cy_s.at[0], cy_r.at[0], y_peer(d))
            to_send(coarse_g.at[0, 0, others], cy_s.at[0])
        forward(1)
        if last:
            finish = pn[cen]
            picked0, near0, picked1, near1 = (finish[k : k + 1] for k in range(4))
            arrive('w_pn', pn_recv.at[pl.ds(1, NCEN - 1)], p_r.at[0])
            for d in range(1, NCEN):
                picked0 = picked0 + pn_recv[d, 0:1, :]
                near0 = jnp.minimum(near0, pn_recv[d, 1:2, :])
                picked1 = picked1 + pn_recv[d, 2:3, :]
                near1 = jnp.minimum(near1, pn_recv[d, 3:4, :])
            gap_g[cen, 0:1, :] = (picked0 - near0) / 32.0
            gap_g[cen, 1:2, :] = (picked1 - near1) / 32.0
            for d in range(1, NCEN):
                remote(gap_g.at[cen], gap_g.at[cen], g_s.at[0], g_r.at[0], c_peer(d))
            to_send(gap_g.at[pl.ds(1, NCEN - 1)], g_s.at[0])
            arrive('w_cy', coarse_g.at[0, 0, others], cy_r.at[0])
            ref = coarse_g.at[core, x]
            for where in (right, left, beyond):
                remote(ref, ref, cx_s.at[0], cx_r.at[0], where)
            to_send(coarse_g.at[0, pl.ds(0, 3)], cx_s.at[0])
        total = jnp.zeros((1, NK), F32)
        for h in range(2):
            arrive('w_gx', fine_g.at[p, h, pl.ds(0, 2)], gx_r.at[p, h, 2])
            for bx in range(NX):
                b = h * NX + bx
                t = fine_g[p, h, bx].reshape(128, NK)
                if last:
                    fine_out[:, b * 128 : (b + 1) * 128] = t.T
                else:
                    low[b * 128 : (b + 1) * 128, :] = t.astype(BF16)
                    total = total + jnp.sum(t * t, axis=0, keepdims=True)
        if not last:
            norm[...] = total

    f_write = pltpu.make_async_copy(fine_out, fine_hbm, out_sem.at[0])
    f_write.start()
    arrive('w_cx', coarse_g.at[0, pl.ds(0, 3)], cx_r.at[0])
    ref = coarse_g.at[core]
    remote(ref, ref, cp_s.at[0], cp_r.at[0], partner)
    to_send(ref, cp_s.at[0])
    arrive('w_gap', gap_g.at[pl.ds(1, NCEN - 1)], g_r.at[0])
    for c in range(NCEN):
        gaps_out[:, c * GP : (c + 1) * GP] = gap_g[c]
    g_write = pltpu.make_async_copy(gaps_out, gaps_hbm, out_sem.at[2])
    g_write.start()
    arrive('w_cp', ref, cp_r.at[0])
    t = jnp.concatenate([coarse_g[c].reshape(NX * NY, 8, 128) for c in range(2)], axis=1).reshape(512, 128).T
    coarse_out[:, 0:512] = t[0:NC]
    coarse_out[:, 512:1024] = t[NC : 2 * NC]
    c_write = pltpu.make_async_copy(coarse_out, coarse_hbm, out_sem.at[1])
    c_write.start()
    with jax.named_scope('w_sends'):
        for copy in sent:
            copy.wait_send()
    for copy in (g_write, f_write, c_write):
        copy.wait()


def coarse_update(parts, counts, coarse):
    total, count = parts[0], counts[0]
    for c in range(1, NCEN):
        total = total + parts[c]
        count = count + counts[c]
    return (total + PRIOR * coarse) / (count + PRIOR)


def write_out(fine, coarse, gaps, fine_hbm, coarse_hbm, gaps_hbm, fine_v, coarse_v, gaps_v, sem):
    through = ((fine, fine_v, fine_hbm), (coarse, coarse_v, coarse_hbm), (gaps, gaps_v, gaps_hbm))
    reads = [pltpu.make_async_copy(src, via, sem.at[0, i]) for i, (src, via, _) in enumerate(through)]
    writes = [pltpu.make_async_copy(via, dst, sem.at[1, i]) for i, (_, via, dst) in enumerate(through)]
    for copy in reads:
        copy.start()
    for read, write in zip(reads, writes):
        read.wait()
        write.start()
    for copy in writes:
        copy.wait()


def on_device(points, fine_assign, fine_start, coarse_start, coarse_assign):
    dma = pltpu.SemaphoreType.DMA
    vmem = pltpu.VMEM
    n = PASSES
    scratch = [
        vmem((NP, D + 128), BF16), vmem((PASSES, NP), jnp.int32), vmem((NK, D), F32), vmem((NC, D), F32),
        vmem((1, NK), jnp.int32), dma((STEPS + 4,)),
        vmem((D, NK), BF16), vmem((1, NK), F32), vmem((CH, NK), F32), vmem((CH, NK), F32),
        vmem((STEPS, 1, CH), F32), vmem((2 * NK, NP + 128), BF16), vmem((NK, 128), F32),
        vmem((n, 2, 128, 128), F32), vmem((n, 2, 64, 128), F32), vmem((n, 2, 64, 128), F32),
        vmem((n, 2, 128, 128), F32), vmem((n, 2, 128, 128), F32), vmem((n, 2, 128, 128), F32),
        vmem((n, 2, 128, 128), F32), vmem((2, 128, 128), F32),
        vmem((n, 2, NY, 16, 128), F32), vmem((n, 2, NY, 16, 128), F32),
        vmem((n, 1, 128), F32), vmem((n, 3, 1, 128), F32), vmem((n, 1, 128), F32), vmem((n, NY, 1, 128), F32),
        vmem((n, 2, NX, NY, 16, 128), F32), vmem((512, 128), F32), vmem((n, NCEN, 16, 128), F32),
        vmem((n, NCEN, 1, 128), F32), vmem((2, 16, 128), F32), vmem((2, NX, NY, 8, 128), F32),
        vmem((NCEN, 4, GP), F32), vmem((NCEN, 4, GP), F32), vmem((NCEN, 2, GP), F32),
        vmem((NK, D), F32), vmem((NC, D), F32), vmem((PASSES, NP), F32), dma((3,)),
        dma((n, 2)), dma((n, 2, 3)), dma((n, 2)), dma((n, 2)), dma((n, 2)), dma((n, 2)), dma((n, 2)), dma((n, 2, 3)),
        *[dma((n,))] * 8, *[dma((1,))] * 10,
    ]
    shapes = (
        jax.ShapeDtypeStruct((NK, D), F32),
        jax.ShapeDtypeStruct((NC, D), F32),
        jax.ShapeDtypeStruct((PASSES, NP), F32),
    )
    outs = pl.pallas_call(
        kernel,
        out_shape=shapes,
        in_specs=[pl.BlockSpec(memory_space=pl.ANY)] * 5,
        out_specs=[pl.BlockSpec(memory_space=pl.ANY)] * 3,
        scratch_shapes=scratch,
        compiler_params=pltpu.CompilerParams(
            collective_id=0, has_side_effects=True, vmem_limit_bytes=67043328
        ),
    )(points, fine_assign, fine_start, coarse_start, coarse_assign.reshape(1, NK))
    return tuple(pl.pallas_call(
        write_out,
        out_shape=shapes,
        in_specs=[pl.BlockSpec(memory_space=pl.ANY)] * 3,
        out_specs=[pl.BlockSpec(memory_space=pl.ANY)] * 3,
        scratch_shapes=[vmem((NK, D), F32), vmem((NC, D), F32), vmem((PASSES, NP), F32), dma((2, 3))],
        compiler_params=pltpu.CompilerParams(vmem_limit_bytes=67043328),
    )(*outs))


def solution(mesh):
    placed = (P("pts", None), P(None, "pts"), P("cen", None), P(), P("cen"))
    return jax.shard_map(
        on_device,
        mesh=mesh,
        in_specs=placed,
        out_specs=(P("cen", None), P(), P(None, "pts")),
        check_vma=False,
    )
```

time: 88.8 us -> 83.8 us (0.944)
  Pallas kernels: 87 us -> 83 us
    pallas_call x1, Pallas kernels: 85 us -> 81 us  [on_device(): pl.pallas_call(kernel, out_shape=shapes, in_specs=[pl.BlockSpec(memory_sp...]
where the time goes in v4:
time: 83.8 us; the launch traced here: 83.6 us
  Pallas kernels  83 us (99%)
    pallas_call x1, Pallas kernels, on_device(): pl.pallas_call(kernel, out_shape=shapes, in_specs=[pl.BlockSpec(memory_sp...  81 us
    pallas_call x1, Pallas kernels, on_device(): pl.pallas_call(write_out, out_shape=shapes, in_specs=[pl.BlockSpec(memory...  1.97 us

profile of v4, /device:TPU:1, one launch (start us, length us, event | category | flops | bytes accessed | tf_op | source)
XLA Modules:
  0.0 83.6 jit_solution(1164851070635236615)
XLA Ops:
  0.6 81.0 %shard_map.76 = (f32[128,1024]{1,0:T(8,128)}, f32[64,1024]{1,0:T(8,128)}, f32[2,4096]{1,0:T(2,128)}) custom-call(bf16[4096,1024]{1,0:T(8,128)(2,1)} %points.1, s32[2,4096]{1,0:T(2,128)} %assign.1, f32[128,1024]{1,0:T(8,128)} %fine_start.1, f32[64,1024]{1,0:T(8,128)} %coarse_start.1, s32[1,128]{1,0:T(1,128)} %bitcast.1), custom_call_target="tpu_custom_call" | custom-call | tf_op jit(solution)/shard_map/pallas_call | solution.py:410
  81.7 2.0 %shard_map.77 = (f32[128,1024]{1,0:T(8,128)}, f32[64,1024]{1,0:T(8,128)}, f32[2,4096]{1,0:T(2,128)}) custom-call(f32[128,1024]{1,0:T(8,128)} %get-tuple-element.6.fine, f32[64,1024]{1,0:T(8,128)} %get-tuple-element.7.coarse, f32[2,4096]{1,0:T(2,128)} %get-tuple-element.8.gaps), custom_call_target="tpu_custom_call" | custom-call | tf_op jit(solution)/shard_map/pallas_call | solution.py:420

commit v5 on v4

--- a/solution.py
+++ b/solution.py
@@ -159,8 +159,8 @@
         select(STEPS - 2, prod_a)
         select(STEPS - 1, prod_b)
 
-    def pair(first, second, h):
-        cols = [pl.ds(pl.multiple_of(h * 512 + b * 128, 128), 128) for b in (first, second)]
+    def pair(*which):
+        cols = [pl.ds(pl.multiple_of(h * 512 + b * 128, 128), 128) for b, h in which]
         rhs = jnp.concatenate([xv[:, cols[0]], xv[:, cols[1]]], axis=1)
         both = jnp.dot(wv[:, 0:NP], rhs, preferred_element_type=F32)
         return (both[:NK] + both[NK:]).T
@@ -182,29 +182,25 @@
         cnt_s[p] = cnt
         LO, HI = pl.ds(0, 64), pl.ds(64, 64)
 
-        for h in range(2):
+        t = pair((x_far, 0), (x_far, 1))
+        far[p, 0] = t[:128]
+        far[p, 1] = t[128:]
+        if p == 0:
+            with jax.named_scope('w_barrier'):
+                pl.semaphore_wait(barrier, 3 + (NY - 1) + (NCEN - 1))
+        for h in range(2):
+            remote(far.at[p, h, LO], hop_r.at[p, h], rs_s.at[p, h], rs_r.at[p, h, 0], right)
+            remote(far.at[p, h, HI], hop_l.at[p, h], rs_s.at[p, h], rs_r.at[p, h, 1], left)
+        for k, where in enumerate((right, left, beyond)):
+            remote(cnt_s.at[p], cnt_x.at[p, k], nx_s.at[p], nx_r.at[p], where)
+        to_send(cnt_x.at[p], nx_s.at[p])
+        for h in range(2):
+            t = pair((x_right, h), (x_left, h))
+            blk_r[p, h] = t[:128]
+            blk_l[p, h] = t[128:]
             ss, rr = rs_s.at[p, h], rs_r.at[p, h, 2]
-            t = pair(x_far, x_right, h)
-            far[p, h] = t[:128]
-            blk_r[p, h] = t[128:]
-            if p == 0 and h == 0:
-                with jax.named_scope('w_barrier'):
-                    pl.semaphore_wait(barrier, 3 + (NY - 1) + (NCEN - 1))
-            remote(far.at[p, h, LO], hop_r.at[p, h], ss, rs_r.at[p, h, 0], right)
-            remote(far.at[p, h, HI], hop_l.at[p, h], ss, rs_r.at[p, h, 1], left)
             remote(blk_r.at[p, h, HI], got_l.at[p, h, HI], ss, rr, right)
-            if h == 0:
-                for k, where in enumerate((right, left, beyond)):
-                    remote(cnt_s.at[p], cnt_x.at[p, k], nx_s.at[p], nx_r.at[p], where)
-                to_send(cnt_x.at[p], nx_s.at[p])
-            t = pair(x_left, x, h)
-            blk_l[p, h] = t[:128]
-            own_s[h] = t[128:]
             remote(blk_l.at[p, h, LO], got_r.at[p, h, LO], ss, rr, left)
-        if last:
-            for d in range(1, NCEN):
-                remote(pn.at[(cen + d) % NCEN], pn_recv.at[d], p_s.at[0], p_r.at[0], c_peer(d))
-            to_send(pn_recv.at[pl.ds(1, NCEN - 1)], p_s.at[0])
         for h in range(2):
             ss, rr = rs_s.at[p, h], rs_r.at[p, h, 2]
             arrive(f'w_hop{h}', hop_r.at[p, h], rs_r.at[p, h, 0])
@@ -221,6 +217,13 @@
             remote(cnt_m.at[p], cnt_y.at[p, d], ny_s.at[p], ny_r.at[p], y_peer(d))
         others = pl.ds(1, NY - 1)
         to_send(cnt_y.at[p, others], ny_s.at[p])
+        if last:
+            for d in range(1, NCEN):
+                remote(pn.at[(cen + d) % NCEN], pn_recv.at[d], p_s.at[0], p_r.at[0], c_peer(d))
+            to_send(pn_recv.at[pl.ds(1, NCEN - 1)], p_s.at[0])
+        t = pair((x, 0), (x, 1))
+        own_s[0] = t[:128]
+        own_s[1] = t[128:]
         for h in range(2):
             arrive(f'w_rsx{h}', fine_g.at[p, h, pl.ds(0, 2)], rs_r.at[p, h, 2])
             ysend[p, h] = (own_s[h] + got_l[p, h] + got_r[p, h]).reshape(NY, 16, 128)

time: 83.8 us -> 81 us (0.967)
  Pallas kernels: 83 us -> 80.3 us
    pallas_call x1, Pallas kernels: 81 us -> 78.3 us  [on_device(): pl.pallas_call(kernel, out_shape=shapes, in_specs=[pl.BlockSpec(memory_sp...]
where the time goes in v5:
time: 81 us; the launch traced here: 80.9 us
  Pallas kernels  80.3 us (99%)
    pallas_call x1, Pallas kernels, on_device(): pl.pallas_call(kernel, out_shape=shapes, in_specs=[pl.BlockSpec(memory_sp...  78.3 us
    pallas_call x1, Pallas kernels, on_device(): pl.pallas_call(write_out, out_shape=shapes, in_specs=[pl.BlockSpec(memory...  1.97 us

profile of v5, /device:TPU:1, one launch (start us, length us, event | category | flops | bytes accessed | tf_op | source)
XLA Modules:
  0.0 80.9 jit_solution(11546525044153374498)
XLA Ops:
  0.6 78.3 %shard_map.76 = (f32[128,1024]{1,0:T(8,128)}, f32[64,1024]{1,0:T(8,128)}, f32[2,4096]{1,0:T(2,128)}) custom-call(bf16[4096,1024]{1,0:T(8,128)(2,1)} %points.1, s32[2,4096]{1,0:T(2,128)} %assign.1, f32[128,1024]{1,0:T(8,128)} %fine_start.1, f32[64,1024]{1,0:T(8,128)} %coarse_start.1, s32[1,128]{1,0:T(1,128)} %bitcast.1), custom_call_target="tpu_custom_call" | custom-call | tf_op jit(solution)/shard_map/pallas_call | solution.py:413
  78.9 2.0 %shard_map.77 = (f32[128,1024]{1,0:T(8,128)}, f32[64,1024]{1,0:T(8,128)}, f32[2,4096]{1,0:T(2,128)}) custom-call(f32[128,1024]{1,0:T(8,128)} %get-tuple-element.6.fine, f32[64,1024]{1,0:T(8,128)} %get-tuple-element.7.coarse, f32[2,4096]{1,0:T(2,128)} %get-tuple-element.8.gaps), custom_call_target="tpu_custom_call" | custom-call | tf_op jit(solution)/shard_map/pallas_call | solution.py:423

commit v6 on v5

--- a/solution.py
+++ b/solution.py
@@ -154,7 +154,8 @@
             return carry
 
         multiply(0, prod_a)
-        lax.fori_loop(0, STEPS // 2 - 1, body, 0)
+        for i in range(STEPS // 2 - 1):
+            body(i, 0)
         multiply(STEPS - 1, prod_b)
         select(STEPS - 2, prod_a)
         select(STEPS - 1, prod_b)

time: 81 us -> 80.1 us (0.989)
  Pallas kernels: 80.3 us -> 79.3 us
    pallas_call x1, Pallas kernels: 78.3 us -> 77.4 us  [on_device(): pl.pallas_call(kernel, out_shape=shapes, in_specs=[pl.BlockSpec(memory_sp...]
where the time goes in v6:
time: 80.1 us; the launch traced here: 80 us
  Pallas kernels  79.3 us (99%)
    pallas_call x1, Pallas kernels, on_device(): pl.pallas_call(kernel, out_shape=shapes, in_specs=[pl.BlockSpec(memory_sp...  77.4 us
    pallas_call x1, Pallas kernels, on_device(): pl.pallas_call(write_out, out_shape=shapes, in_specs=[pl.BlockSpec(memory...  1.97 us

profile of v6, /device:TPU:1, one launch (start us, length us, event | category | flops | bytes accessed | tf_op | source)
XLA Modules:
  0.0 80.0 jit_solution(18367742569312176340)
XLA Ops:
  0.6 77.4 %shard_map.76 = (f32[128,1024]{1,0:T(8,128)}, f32[64,1024]{1,0:T(8,128)}, f32[2,4096]{1,0:T(2,128)}) custom-call(bf16[4096,1024]{1,0:T(8,128)(2,1)} %points.1, s32[2,4096]{1,0:T(2,128)} %assign.1, f32[128,1024]{1,0:T(8,128)} %fine_start.1, f32[64,1024]{1,0:T(8,128)} %coarse_start.1, s32[1,128]{1,0:T(1,128)} %bitcast.1), custom_call_target="tpu_custom_call" | custom-call | tf_op jit(solution)/shard_map/pallas_call | solution.py:414
  78.0 2.0 %shard_map.77 = (f32[128,1024]{1,0:T(8,128)}, f32[64,1024]{1,0:T(8,128)}, f32[2,4096]{1,0:T(2,128)}) custom-call(f32[128,1024]{1,0:T(8,128)} %get-tuple-element.6.fine, f32[64,1024]{1,0:T(8,128)} %get-tuple-element.7.coarse, f32[2,4096]{1,0:T(2,128)} %get-tuple-element.8.gaps), custom_call_target="tpu_custom_call" | custom-call | tf_op jit(solution)/shard_map/pallas_call | solution.py:424
